TPU v7x, 32 devices: a whole 2x2x4 slice. The times are simulated.
32 devices in a mesh: samp: 8 (over z, x), win: 1, snp: 4 (over y, core).
Axes of the slice: x: 2, y: 2, z: 4, core: 2. Of those that a mesh axis runs over, the one named last changes fastest.
Arguments:
- dosages: bfloat16 [4096, 4096], P('samp', ('win', 'snp')), may hold values from 0 to 2
Outputs:
- r_squared: float32 [1, 4096, 4096], P('win', 'samp', 'snp')
- band_r_squared: float32 [1, 1024, 4096], P('win', 'samp', 'snp')
All inputs are finite; a program needn't handle non-finite values.
Results may differ from a plain program's by a relative error of at most 0.0003.
Values may be sent and summed in bfloat16 or wider, within the bound.
No kernel may reach another device: no remote copies, remote signals or barrier semaphores. Data moves between devices by JAX's collectives and lax.ppermute only.
A program may use at most 128 MiB of HBM per device.

v0:
```python
import jax
import jax.numpy as jnp
from jax import lax
from jax.sharding import PartitionSpec as P

OV = 1024


var_floor = 0.05


def passed_along(shard, axis, by):
    devices = lax.axis_size(axis)
    return lax.ppermute(shard, axis, [(i, (i + by) % devices) for i in range(devices)])


def squared_corr(gram, col_sum, col_sq, row_sum, row_sq, count):
    col_mean = col_sum / count
    row_mean = row_sum / count
    col_var = jnp.maximum(col_sq / count - col_mean * col_mean, var_floor)
    row_var = jnp.maximum(row_sq / count - row_mean * row_mean, var_floor)
    covar = gram / count - col_mean[:, None] * row_mean[None, :]
    return covar * covar / (col_var[:, None] * row_var[None, :])


def column_stats(block):
    return (
        jnp.sum(block, axis=0, dtype=jnp.float32),
        jnp.sum(jnp.square(block.astype(jnp.float32)), axis=0),
    )


def pair_sums(columns, own_rows):
    return lax.dot_general(
        columns, own_rows, (((0,), (0,)), ((), ())), preferred_element_type=jnp.float32
    )


def shards(dosages):
    samples_here = dosages.shape[0]
    block_width = dosages.shape[1]
    shard_count = lax.axis_size("samp")
    count = jnp.float32(samples_here * shard_count)
    whole = lax.all_gather(dosages, "snp", axis=1, tiled=True)
    window_width = whole.shape[1]
    band = passed_along(whole[:, :OV], "win", -1)
    own_sum, own_sq = column_stats(dosages)
    total_sum, total_sq = lax.psum((own_sum, own_sq), "samp")
    win_sum, win_sq = (
        lax.all_gather(total_sum, "snp", axis=0, tiled=True),
        lax.all_gather(total_sq, "snp", axis=0, tiled=True),
    )
    next_sum, next_sq = passed_along((win_sum[:OV], win_sq[:OV]), "win", -1)
    win_cols = window_width // shard_count
    band_cols = OV // shard_count
    merged = jnp.concatenate(
        (
            whole.reshape(samples_here, shard_count, win_cols),
            band.reshape(samples_here, shard_count, band_cols),
        ),
        axis=2,
    ).reshape(samples_here, shard_count * (win_cols + band_cols))
    summed = lax.psum_scatter(pair_sums(merged, dosages), "samp", scatter_dimension=0, tiled=True)
    win_gram = summed[:win_cols]
    band_gram = summed[win_cols:]
    col_index = lax.axis_index("samp")
    row_index = lax.axis_index("snp")
    row_sum = lax.dynamic_slice_in_dim(win_sum, row_index * block_width, block_width, 0)
    row_sq = lax.dynamic_slice_in_dim(win_sq, row_index * block_width, block_width, 0)
    col_sum = lax.dynamic_slice_in_dim(win_sum, col_index * win_cols, win_cols, 0)
    col_sq = lax.dynamic_slice_in_dim(win_sq, col_index * win_cols, win_cols, 0)
    band_sum = lax.dynamic_slice_in_dim(next_sum, col_index * band_cols, band_cols, 0)
    band_sq = lax.dynamic_slice_in_dim(next_sq, col_index * band_cols, band_cols, 0)
    whole_out = squared_corr(win_gram, col_sum, col_sq, row_sum, row_sq, count)
    band_out = squared_corr(band_gram, band_sum, band_sq, row_sum, row_sq, count)
    return (whole_out[None], band_out[None])


def solution(mesh):
    return jax.shard_map(
        shards,
        mesh=mesh,
        in_specs=(P("samp", ("win", "snp")),),
        out_specs=(P("win", "samp", "snp"), P("win", "samp", "snp")),
        check_vma=False,
    )
```

profile of v0, /device:TPU:0, one launch (start us, length us, event | category | flops | bytes accessed | tf_op | source)
XLA Modules:
  0.0 419.4 jit_solution(9305339508099588703)
XLA Ops:
  7.2 0.0 all-gather.2.cloned.1.call-start
  7.2 0.7 all-gather.2.cloned.1.call-update
  7.9 0.0 reduce-scatter.2.cloned.1.call-start
  7.9 38.8 %all-gather.2.cloned.1.call-done = bf16[512,4096]{1,0:T(8,128)(2,1)} async-done(((bf16[512,1024]{1,0:T(8,128)(2,1)}), bf16[512,4096]{1,0:T(8,128)(2,1)}) %all-gather.2.cloned.1.call-update) | async-done | bytes 4194320 | tf_op jit(solution)/shard_map/all_gather | solution.py:44
  46.8 1.3 slice.20
  48.0 0.1 collective-permute-start
  48.1 4.4 %copy.3 = bf16[64,8,8,512]{3,2,1,0:T(8,128)(2,1)S(1)} copy(bf16[64,8,8,512]{3,1,2,0:T(8,128)(2,1)} %bitcast.14) | data formatting | bytes 8388608
  52.5 0.0 collective-permute-done
  52.6 0.3 copy.4
  52.8 0.5 pad_maximum_fusion
  53.3 0.0 copy-start
  53.3 1.2 copy.5
  54.5 0.0 copy-done
  54.5 9.9 %fusion.10 = f32[5120,1024]{1,0:T(8,128)} fusion(bf16[512,5120]{1,0:T(8,128)(2,1)S(1)} %bitcast.15, bf16[512,1024]{1,0:T(8,128)(2,1)S(1)} %copy-done), kind=kOutput, calls=%fused_computation.21 | convolution fusion | flops 5368709120 | bytes 27262976 | tf_op jit(solution)/shard_map/dot_general | solution.py:34
  64.4 0.0 reduce-scatter.2.cloned.1.call-update
  64.4 0.3 convert_reduce_fusion
  64.8 22.7 %all-reduce = (f32[1024]{0:T(1024)S(1)}, f32[1024]{0:T(1024)S(1)}) all-reduce(f32[1024]{0:T(1024)S(1)} %get-tuple-element.3, f32[1024]{0:T(1024)S(1)} %get-tuple-element.2), channel_id=1, replica_groups=mesh['samp'=8,'win'=1,'snp'=4] {'samp'}, use_global_device_ids=true, to_apply=%region_4.0 | all-reduce | flops 2048 | bytes 16384 | tf_op jit(solution)/shard_map/psum | solution.py:48
  87.5 5.2 %all_gather.10 = f32[4096]{0:T(1024)S(1)} all-gather(f32[1024]{0:T(1024)S(1)} %get-tuple-element.5), channel_id=1, replica_groups=mesh['samp'=8,'win'=1,'snp'=4] {'snp'}, dimensions={0}, use_global_device_ids=true | all-gather | bytes 20480 | tf_op jit(solution)/shard_map/all_gather | solution.py:50
  92.7 5.2 %all_gather.11 = f32[4096]{0:T(1024)S(1)} all-gather(f32[1024]{0:T(1024)S(1)} %get-tuple-element.4), channel_id=1, replica_groups=mesh['samp'=8,'win'=1,'snp'=4] {'snp'}, dimensions={0}, use_global_device_ids=true | all-gather | bytes 20480 | tf_op jit(solution)/shard_map/all_gather | solution.py:51
  97.9 0.0 collective-permute-start.1
  97.9 0.0 collective-permute-start.2
  97.9 0.1 dynamic-slice_multiply_fusion.1
  98.0 0.0 collective-permute-done.1
  98.0 0.0 collective-permute-done.2
  98.0 0.1 dynamic-slice_multiply_fusion.2
  98.1 308.9 %reduce-scatter.2.cloned.1.call-done = f32[640,1024]{1,0:T(8,128)} async-done(((f32[5120,1024]{1,0:T(8,128)}), f32[640,1024]{1,0:T(8,128)}) %reduce-scatter.2.cloned.1.call-update) | async-done | bytes 2621456 | tf_op jit(solution)/shard_map/reduce_scatter | solution.py:63
  407.0 3.5 fusion.4
  410.5 2.0 fusion.8
  (1 shorter events, 0.0 us)
Async XLA Ops:
  7.2 39.6 %all-gather.2.cloned.1.call-start = ((), (), s32[]{:S(2)}) async-start(), calls=%async_computation.1 | async-start | bytes 5242880 | tf_op jit(solution)/shard_map/all_gather | solution.py:44
  7.9 399.1 %reduce-scatter.2.cloned.1.call-start = ((), (), s32[]{:S(2)}) async-start(), calls=%async_computation.2 | async-start | bytes 23592960 | tf_op jit(solution)/shard_map/reduce_scatter | solution.py:63
  48.0 4.5 %collective-permute-start = (bf16[512,1024]{1,0:T(8,128)(2,1)S(1)}, bf16[512,1024]{1,0:T(8,128)(2,1)S(1)}, u32[]{:S(2)}, u32[]{:S(2)}) collective-permute-start(bf16[512,1024]{1,0:T(8,128)(2,1)S(1)} %slice.20), channel_id=1, source_target_pairs={{0,0},{1,1},{2,2},{3,3},{4,4},{5,5},{6,6},{7,7},{8,8},{9,9},{10,10... | collective-permute-start | bytes 3145736 | tf_op jit(solution)/shard_map/ppermute | solution.py:14
  53.3 1.2 copy-start
  97.9 0.1 collective-permute-start.1
  97.9 0.1 collective-permute-start.2
Sparse Core Ops, SparseCore 0:
  9.5 37.1 all-gather.1
  64.6 342.4 reduce-scatter.1
where the time goes:
time: 420 us; the launch traced here: 419 us
  waiting for transfers between devices  348 us (83%)
  blocking collectives  33.1 us (8%)
  between operations  14.1 us (3%)
  matrix products  9.9 us (2%)
  local copies, waits for them, and re-layouts  7.19 us (2%)
  other arithmetic  6.47 us (2%)
    reduce_scatter x1, waiting for transfers between devices, shards(): lax.psum_scatter(pair_sums(merged, dosages), 'samp', scatter_dimension=0,...  309 us
    all_gather x1, waiting for transfers between devices, shards(): whole = lax.all_gather(dosages, 'snp', axis=1, tiled=True)  38.8 us
    psum x1, blocking collectives, shards(): total_sum, total_sq = lax.psum((own_sum, own_sq), 'samp')  22.7 us
    dot_general x1, matrix products, pair_sums(): lax.dot_general(columns, own_rows, (((0,), (0,)), ((), ())), preferred_el...  9.9 us
  transfers between devices with their start and end apart: 5, of which 2 were waited for; matrix products, arithmetic and copies ran while one was open for 1% of the time, Pallas kernels for 0%

commit v1 on v0

--- a/solution.py
+++ b/solution.py
@@ -1,12 +1,259 @@
+import functools
+
 import jax
 import jax.numpy as jnp
 from jax import lax
+from jax.experimental import pallas as pl
+from jax.experimental.pallas import tpu as pltpu
 from jax.sharding import PartitionSpec as P
 
+
 OV = 1024
 
 
 var_floor = 0.05
+
+
+def ring_pairs(size, step):
+    order = list(range(0, size, 2)) + list(range(1, size, 2))[::-1]
+    return [(order[i], order[(i + step) % size]) for i in range(size)]
+
+
+def ring_chunks(own):
+    size = lax.axis_size("samp")
+    half = own.shape[0] // 2
+    ahead = ring_pairs(size, 1)
+    back = ring_pairs(size, -1)
+    fore = [own[:half], own[half:]]
+    aft = [own[half:], own[:half]]
+    groups = [[own[:half], own[half:]]]
+    steps = size - 1
+    pending = []
+    for step in range(steps):
+        lane = step % 2
+        fore[lane] = lax.ppermute(fore[lane], "samp", ahead)
+        aft[lane] = lax.ppermute(aft[lane], "samp", back)
+        pending += [fore[lane], aft[lane]]
+        if lane == 1 and step < 4 or step >= 4:
+            groups.append(pending)
+            pending = []
+    return groups
+
+
+def parts_of(where, width, win_cols):
+    return (
+        (where[2], where[3], slice(0, win_cols)),
+        (where[4], where[5], slice(win_cols, width)),
+    )
+
+
+def pick_columns(where, *refs, win_cols):
+    out = refs[-1]
+    width = out.shape[1]
+    for i, chunk in enumerate(refs[:-1]):
+        for at, (_, _, part) in zip((where[0], where[1]), parts_of(where, width, win_cols)):
+            at = pl.ds(pl.multiple_of(at, 128), part.stop - part.start)
+            out[i, part] = chunk[:, at].T
+
+
+def pick_core(where, mine, theirs, out, win_cols):
+    half = out.shape[0]
+    base = where[6] * half
+    for core, _, part in parts_of(where, out.shape[1], win_cols):
+
+        @pl.when(core == where[6])
+        def _():
+            out[:, part] = mine[pl.ds(base, half), part]
+
+        @pl.when(core != where[6])
+        def _():
+            out[:, part] = theirs[pl.ds(base, half), part]
+
+
+def local_call(body, shape, operands, win_cols):
+    vmem = pl.BlockSpec(memory_space=pltpu.VMEM)
+    smem = pl.BlockSpec(memory_space=pltpu.SMEM)
+    return pl.pallas_call(
+        functools.partial(body, win_cols=win_cols),
+        out_shape=jax.ShapeDtypeStruct(shape, jnp.bfloat16),
+        in_specs=[smem] + [vmem] * (len(operands) - 1),
+        out_specs=vmem,
+        compiler_params=pltpu.CompilerParams(vmem_limit_bytes=8 << 20),
+    )(*operands)
+
+
+def wanted_rows(group, where, win_cols, band_cols):
+    shape = (len(group), win_cols + band_cols, group[0].shape[0])
+    mine = local_call(pick_columns, shape, (where, *group), win_cols)
+    swap = [(0, 1), (1, 0), (2, 3), (3, 2)]
+    across = [(0, 2), (1, 3), (2, 0), (3, 1)]
+    theirs = lax.ppermute(mine, "snp", swap)
+    half = (len(group) // 2,) + shape[1:]
+    sent = local_call(pick_core, half, (where, mine, theirs), win_cols)
+    came = lax.ppermute(sent, "snp", across)
+    other = lax.ppermute(came, "snp", swap)
+    return mine, theirs, came, other
+
+
+def gather_rows(where, pieces, slab, win_cols):
+    mine, theirs, came, other = pieces
+    half = slab.shape[0] // 2
+    for core, pair, part in parts_of(where, slab.shape[1], win_cols):
+        near = pair == where[7]
+
+        @pl.when(near & (core == where[6]))
+        def _():
+            slab[:, part] = mine[:, part]
+
+        @pl.when(near & (core != where[6]))
+        def _():
+            slab[:, part] = theirs[:, part]
+
+        @pl.when(jnp.logical_not(near) & (where[6] == 0))
+        def _():
+            slab[:half, part] = came[:, part]
+            slab[half:, part] = other[:, part]
+
+        @pl.when(jnp.logical_not(near) & (where[6] == 1))
+        def _():
+            slab[:half, part] = other[:, part]
+            slab[half:, part] = came[:, part]
+
+
+def add_stats(cols, slab, col_before, row_before, col_out, row_out):
+    width = cols[0].shape[1]
+    for out, before, op in ((0, 0, lambda v: v), (8, 8, lambda v: v * v)):
+        total = None if col_before is None else col_before[before : before + 8]
+        for col in cols:
+            wide = op(col[...].astype(jnp.float32))
+            part = jnp.sum(wide.reshape(-1, 8, width), axis=0)
+            total = part if total is None else total + part
+        col_out[out : out + 8] = total
+    for out, op in ((0, lambda v: v), (1, lambda v: v * v)):
+        total = None if row_before is None else row_before[out]
+        for i in range(slab.shape[0]):
+            wide = op(slab[i].astype(jnp.float32))
+            for j in range(0, wide.shape[1], 128):
+                part = wide[:, j : j + 128]
+                total = part if total is None else total + part
+        row_out[out] = total
+
+
+def add_sums(cols, slab, at, before):
+    total = before
+    for i, col in enumerate(cols):
+        part = jnp.dot(slab[i], col[:, at], preferred_element_type=jnp.float32)
+        total = part if total is None else total + part
+    return total
+
+
+def first_sums(where, *refs, size, first, win_cols):
+    cols, pieces = refs[:size], refs[size : size + 4]
+    before = (None, None, None) if first else refs[size + 4 : size + 7]
+    gram, col_out, row_out, slab = refs[-4:]
+    gather_rows(where, pieces, slab, win_cols)
+    add_stats(cols, slab, before[1], before[2], col_out, row_out)
+    tile = 256
+
+    def columns(j, carry):
+        at = pl.ds(pl.multiple_of(j * tile, tile), tile)
+        gram[:, at] = add_sums(cols, slab, at, None if first else before[0][:, at])
+        return carry
+
+    lax.fori_loop(0, gram.shape[1] // tile, columns, 0)
+
+
+def last_sums(where, *refs, size, count, win_cols):
+    cols, pieces = refs[:size], refs[size : size + 4]
+    before = refs[size + 4 : size + 7]
+    win_out, band_out, slab, col_stats, row_stats = refs[-5:]
+    step = pl.program_id(0)
+
+    def moments(total, square, axis):
+        mean = jnp.sum(total, axis=axis, keepdims=True) / count
+        square = jnp.sum(square, axis=axis, keepdims=True) / count
+        return mean, 1.0 / jnp.maximum(square - mean * mean, var_floor)
+
+    @pl.when(step == 0)
+    def _():
+        gather_rows(where, pieces, slab, win_cols)
+        add_stats(cols, slab, before[1], before[2], col_stats, row_stats)
+        mean, inverse = moments(row_stats[0], row_stats[1], 1)
+        row_stats[0] = jnp.broadcast_to(mean, row_stats.shape[1:])
+        row_stats[1] = jnp.broadcast_to(inverse, row_stats.shape[1:])
+        mean, inverse = moments(col_stats[0:8], col_stats[8:16], 0)
+        col_stats[0:1] = mean
+        col_stats[1:2] = inverse
+
+    tile = win_out.shape[1]
+    at = pl.ds(pl.multiple_of(step * tile, tile), tile)
+    total = add_sums(cols, slab, at, before[0][:, at])
+    col_mean, col_inv = col_stats[0:1, at], col_stats[1:2, at]
+    for j in range(0, tile, 128):
+        part = slice(j, j + 128)
+        covar = total[:, part] * (1.0 / count) - row_stats[0] * col_mean[:, part]
+        ratio = covar * covar * (row_stats[1] * col_inv[:, part])
+        win_out[:, part] = ratio[:win_cols]
+        band_out[:, part] = ratio[win_cols:]
+
+
+def summed(where, group, rows, before, last, count, win_cols):
+    width = group[0].shape[1]
+    row_width = rows[0].shape[1]
+    operands = [where, *group, *rows] + ([] if before is None else list(before))
+    gram = (row_width, width)
+    sums = [gram, (16, width), (2, row_width, 128)]
+    slab = pltpu.VMEM(rows[0].shape, jnp.bfloat16)
+    vmem = pl.BlockSpec(memory_space=pltpu.VMEM)
+    smem = pl.BlockSpec(memory_space=pltpu.SMEM)
+    if last:
+        tile = 256
+        body = functools.partial(last_sums, size=len(group), count=count, win_cols=win_cols)
+        shapes = [(win_cols, width), (row_width - win_cols, width)]
+        layout = dict(
+            grid=(width // tile,),
+            out_specs=[pl.BlockSpec((s[0], tile), lambda j: (0, j)) for s in shapes],
+            scratch_shapes=[slab] + [pltpu.VMEM(s, jnp.float32) for s in sums[1:]],
+        )
+    else:
+        first = before is None
+        body = functools.partial(first_sums, size=len(group), first=first, win_cols=win_cols)
+        shapes = sums
+        given = len(operands) - 3
+        layout = dict(
+            out_specs=[vmem] * 3,
+            scratch_shapes=[slab],
+            input_output_aliases={} if first else {given + i: i for i in range(3)},
+        )
+    return pl.pallas_call(
+        body,
+        out_shape=[jax.ShapeDtypeStruct(s, jnp.float32) for s in shapes],
+        in_specs=[smem] + [vmem] * (len(operands) - 1),
+        compiler_params=pltpu.CompilerParams(vmem_limit_bytes=16 << 20),
+        **layout,
+    )(*operands)
+
+
+def shards(dosages):
+    shard_count = lax.axis_size("samp")
+    count = float(dosages.shape[0] * shard_count)
+    width = dosages.shape[1]
+    win_cols = width * lax.axis_size("snp") // shard_count
+    band_cols = OV // shard_count
+    samp, block = lax.axis_index("samp"), lax.axis_index("snp")
+    row_at, band_at = samp * win_cols, samp * band_cols
+    row_block, band_block = row_at // width, band_at // width
+    where = jnp.stack(
+        [row_at % width, band_at % width]
+        + [row_block % 2, row_block // 2, band_block % 2, band_block // 2, block % 2, block // 2]
+    ).astype(jnp.int32)
+    groups = ring_chunks(dosages)
+    rows = [wanted_rows(g, where, win_cols, band_cols) for g in groups]
+    total = None
+    for i, (group, row) in enumerate(zip(groups, rows)):
+        last = i == len(groups) - 1
+        total = summed(where, group, row, total, last, count, win_cols)
+    return (total[0][None], total[1][None])
 
 
 def passed_along(shard, axis, by):
@@ -36,7 +283,7 @@
     )
 
 
-def shards(dosages):
+def shards_by_sums(dosages):
     samples_here = dosages.shape[0]
     block_width = dosages.shape[1]
     shard_count = lax.axis_size("samp")
@@ -77,8 +324,9 @@
 
 
 def solution(mesh):
+    near = mesh.shape["snp"] == 4 and mesh.shape["win"] == 1 and mesh.shape["samp"] == 8
     return jax.shard_map(
-        shards,
+        shards if near else shards_by_sums,
         mesh=mesh,
         in_specs=(P("samp", ("win", "snp")),),
         out_specs=(P("win", "samp", "snp"), P("win", "samp", "snp")),

time: 420 us -> 166 us (0.40)
  waiting for transfers between devices: 348 us -> 103 us
  blocking collectives: 33.1 us -> 0 us
  Pallas kernels: 0 us -> 31.5 us
  starting transfers between devices: 0.15 us -> 28.6 us
  between operations: 14.1 us -> 0.91 us
  matrix products: 9.9 us -> 0 us
  other arithmetic: 6.47 us -> 0 us
  local copies, waits for them, and re-layouts: 7.19 us -> 1.36 us
    reduce_scatter x1 -> x0, waiting for transfers between devices: 309 us -> none  [shards(): lax.psum_scatter(pair_sums(merged, dosages), 'samp', scatter_dimension=0,...]
    ppermute x3 -> x32, waiting for transfers between devices: 0.01 us -> 103 us  [the longest x7 47 us: ring_chunks(): fore[lane] = lax.ppermute(fore[lane], 'samp', ahead)]
    all_gather x1 -> x0, waiting for transfers between devices: 38.8 us -> none  [shards(): whole = lax.all_gather(dosages, 'snp', axis=1, tiled=True)]
    pallas_call x0 -> x18, Pallas kernels: none -> 31.5 us  [the longest x6 21.7 us: summed(): pl.pallas_call(body, out_shape=[jax.ShapeDtypeStruct(s, jnp.float32) for...]
    ppermute x3 -> x32, starting transfers between devices: 0.07 us -> 28.6 us  [the longest x7 13.8 us: ring_chunks(): fore[lane] = lax.ppermute(fore[lane], 'samp', ahead)]
    psum x1 -> x0, blocking collectives: 22.7 us -> none  [shards(): total_sum, total_sq = lax.psum((own_sum, own_sq), 'samp')]
    all_gather x2 -> x0, blocking collectives: 10.4 us -> none  [the longest x1 5.21 us: shards(): lax.all_gather(total_sum, 'snp', axis=0, tiled=True)]
    dot_general x1 -> x0, matrix products: 9.9 us -> none  [pair_sums(): lax.dot_general(columns, own_rows, (((0,), (0,)), ((), ())), preferred_el...]
  transfers between devices with their start and end apart: 5 -> 32, of which waited for: 2 -> 15; matrix products, arithmetic and copies ran while one was open for 1% -> 0% of each run, Pallas kernels for 0% -> 17%
where the time goes in v1:
time: 166 us; the launch traced here: 165 us
  waiting for transfers between devices  103 us (62%)
  Pallas kernels  31.5 us (19%)
  starting transfers between devices  28.6 us (17%)
    ppermute x7, waiting for transfers between devices, ring_chunks(): fore[lane] = lax.ppermute(fore[lane], 'samp', ahead)  47 us
    ppermute x6, waiting for transfers between devices, wanted_rows(): came = lax.ppermute(sent, 'snp', across)  43.9 us
    pallas_call x6, Pallas kernels, summed(): pl.pallas_call(body, out_shape=[jax.ShapeDtypeStruct(s, jnp.float32) for...  21.7 us
    ppermute x7, starting transfers between devices, ring_chunks(): fore[lane] = lax.ppermute(fore[lane], 'samp', ahead)  13.8 us
    ppermute x7, waiting for transfers between devices, ring_chunks(): aft[lane] = lax.ppermute(aft[lane], 'samp', back)  12.1 us
    pallas_call x12, Pallas kernels, local_call(): pl.pallas_call(functools.partial(body, win_cols=win_cols), out_shape=jax....  9.83 us
    ppermute x6, starting transfers between devices, wanted_rows(): came = lax.ppermute(sent, 'snp', across)  7.42 us
    ppermute x7, starting transfers between devices, ring_chunks(): aft[lane] = lax.ppermute(aft[lane], 'samp', back)  6.43 us
  transfers between devices with their start and end apart: 32, of which 15 were waited for; matrix products, arithmetic and copies ran while one was open for 0% of the time, Pallas kernels for 17%

profile of v1, /device:TPU:0, one launch (start us, length us, event | category | flops | bytes accessed | tf_op | source)
XLA Modules:
  0.0 165.4 jit_solution(7829346767006045542)
XLA Ops:
  1.9 3.1 %collective-permute-start = (bf16[256,1024]{1,0:T(8,128)(2,1)S(1)}, bf16[256,1024]{1,0:T(8,128)(2,1)S(1)}, u32[]{:S(2)}, u32[]{:S(2)}) collective-permute-start(bf16[256,1024]{1,0:T(8,128)(2,1)S(1)} %get-tuple-element.37.refs_0_), channel_id=1, source_target_pairs={{0,8},{8,16},{16,24},{24,28},{28,20},{20,12},{12,4},{4,0},{1,9},{9... | collective-permute-start | bytes 1572872 | tf_op jit(solution)/shard_map/ppermute | solution.py:34
  7.1 10.6 %collective-permute-done.refs_0_ = bf16[256,1024]{1,0:T(8,128)(2,1)S(1)} collective-permute-done((bf16[256,1024]{1,0:T(8,128)(2,1)S(1)}, bf16[256,1024]{1,0:T(8,128)(2,1)S(1)}, u32[]{:S(2)}, u32[]{:S(2)}) %collective-permute-start) | collective-permute-done | bytes 524320 | tf_op jit(solution)/shard_map/ppermute | solution.py:34
  17.7 2.1 %collective-permute-start.1 = (bf16[256,1024]{1,0:T(8,128)(2,1)S(1)}, bf16[256,1024]{1,0:T(8,128)(2,1)S(1)}, u32[]{:S(2)}, u32[]{:S(2)}) collective-permute-start(bf16[256,1024]{1,0:T(8,128)(2,1)S(1)} %collective-permute-done.refs_0_), channel_id=1, source_target_pairs={{0,8},{8,16},{16,24},{24,28},{28,20},{20,12},{12,4},{4,0},{1,9},{9... | collective-permute-start | bytes 1572872 | tf_op jit(solution)/shard_map/ppermute | solution.py:34
  19.8 9.1 %collective-permute-done.11.refs_2_ = bf16[256,1024]{1,0:T(8,128)(2,1)S(1)} collective-permute-done((bf16[256,1024]{1,0:T(8,128)(2,1)S(1)}, bf16[256,1024]{1,0:T(8,128)(2,1)S(1)}, u32[]{:S(2)}, u32[]{:S(2)}) %collective-permute-start.11) | collective-permute-done | bytes 524320 | tf_op jit(solution)/shard_map/ppermute | solution.py:34
  28.9 2.1 %collective-permute-start.12 = (bf16[256,1024]{1,0:T(8,128)(2,1)S(1)}, bf16[256,1024]{1,0:T(8,128)(2,1)}, u32[]{:S(2)}, u32[]{:S(2)}) collective-permute-start(bf16[256,1024]{1,0:T(8,128)(2,1)S(1)} %collective-permute-done.11.refs_2_), channel_id=1, source_target_pairs={{0,8},{8,16},{16,24},{24,28},{28,20},{20,12},{12,4},{4,0},{1,9},{9... | collective-permute-start | bytes 1572872 | tf_op jit(solution)/shard_map/ppermute | solution.py:34
  31.1 1.9 %collective-permute-start.5 = (bf16[256,1024]{1,0:T(8,128)(2,1)}, bf16[256,1024]{1,0:T(8,128)(2,1)}, u32[]{:S(2)}, u32[]{:S(2)}) collective-permute-start(bf16[256,1024]{1,0:T(8,128)(2,1)} %collective-permute-done.4.refs_1_), channel_id=1, source_target_pairs={{0,4},{8,0},{16,8},{24,16},{28,24},{20,28},{12,20},{4,12},{1,5},{9... | collective-permute-start | bytes 1572872 | tf_op jit(solution)/shard_map/ppermute | solution.py:35
  35.4 4.8 %collective-permute-done.1.refs_0_ = bf16[256,1024]{1,0:T(8,128)(2,1)S(1)} collective-permute-done((bf16[256,1024]{1,0:T(8,128)(2,1)S(1)}, bf16[256,1024]{1,0:T(8,128)(2,1)S(1)}, u32[]{:S(2)}, u32[]{:S(2)}) %collective-permute-start.1) | collective-permute-done | bytes 524320 | tf_op jit(solution)/shard_map/ppermute | solution.py:34
  40.2 10.5 %collective-permute-done.12.refs_2_ = bf16[256,1024]{1,0:T(8,128)(2,1)} collective-permute-done((bf16[256,1024]{1,0:T(8,128)(2,1)S(1)}, bf16[256,1024]{1,0:T(8,128)(2,1)}, u32[]{:S(2)}, u32[]{:S(2)}) %collective-permute-start.12) | collective-permute-done | bytes 524320 | tf_op jit(solution)/shard_map/ppermute | solution.py:34
  50.7 1.8 %collective-permute-start.2 = (bf16[256,1024]{1,0:T(8,128)(2,1)S(1)}, bf16[256,1024]{1,0:T(8,128)(2,1)S(1)}, u32[]{:S(2)}, u32[]{:S(2)}) collective-permute-start(bf16[256,1024]{1,0:T(8,128)(2,1)S(1)} %collective-permute-done.1.refs_0_), channel_id=1, source_target_pairs={{0,8},{8,16},{16,24},{24,28},{28,20},{20,12},{12,4},{4,0},{1,9},{9... | collective-permute-start | bytes 1572872 | tf_op jit(solution)/shard_map/ppermute | solution.py:34
  53.9 1.8 %shard_map.36.mine.refs_4_ = bf16[4,640,256]{2,1,0:T(8,128)(2,1)S(1)} custom-call(s32[8]{0:T(128)S(1)} %stack.35.where, bf16[256,1024]{1,0:T(8,128)(2,1)S(1)} %collective-permute-done.1.refs_0_, bf16[256,1024]{1,0:T(8,128)(2,1)} %collective-permute-done.5.refs_1_, bf16[256,1024]{1,0:T(8,128)(2,1)} %collective-permute-done.12.refs_2_, ...), custom_call_target="tpu_custom_call" | custom-call | tf_op jit(solution)/shard_map/pallas_call | solution.py:76
  57.8 7.6 %collective-permute-done.2.refs_0_ = bf16[256,1024]{1,0:T(8,128)(2,1)S(1)} collective-permute-done((bf16[256,1024]{1,0:T(8,128)(2,1)S(1)}, bf16[256,1024]{1,0:T(8,128)(2,1)S(1)}, u32[]{:S(2)}, u32[]{:S(2)}) %collective-permute-start.2) | collective-permute-done | bytes 524320 | tf_op jit(solution)/shard_map/ppermute | solution.py:34
  65.5 1.7 %collective-permute-start.16 = (bf16[256,1024]{1,0:T(8,128)(2,1)}, bf16[256,1024]{1,0:T(8,128)(2,1)S(1)}, u32[]{:S(2)}, u32[]{:S(2)}) collective-permute-start(bf16[256,1024]{1,0:T(8,128)(2,1)} %collective-permute-done.15.refs_3_), channel_id=1, source_target_pairs={{0,4},{8,0},{16,8},{24,16},{28,24},{20,28},{12,20},{4,12},{1,5},{9... | collective-permute-start | bytes 1572872 | tf_op jit(solution)/shard_map/ppermute | solution.py:35
  67.2 3.6 %collective-permute-done.6.refs_1_ = bf16[256,1024]{1,0:T(8,128)(2,1)S(1)} collective-permute-done((bf16[256,1024]{1,0:T(8,128)(2,1)}, bf16[256,1024]{1,0:T(8,128)(2,1)S(1)}, u32[]{:S(2)}, u32[]{:S(2)}) %collective-permute-start.6) | collective-permute-done | bytes 524320 | tf_op jit(solution)/shard_map/ppermute | solution.py:35
  70.8 1.6 collective-permute-start.3
  72.4 4.3 %collective-permute-done.13.refs_0_ = bf16[256,1024]{1,0:T(8,128)(2,1)S(1)} collective-permute-done((bf16[256,1024]{1,0:T(8,128)(2,1)}, bf16[256,1024]{1,0:T(8,128)(2,1)S(1)}, u32[]{:S(2)}, u32[]{:S(2)}) %collective-permute-start.13) | collective-permute-done | bytes 524320 | tf_op jit(solution)/shard_map/ppermute | solution.py:34
  76.7 1.7 %collective-permute-start.7 = (bf16[256,1024]{1,0:T(8,128)(2,1)S(1)}, bf16[256,1024]{1,0:T(8,128)(2,1)S(1)}, u32[]{:S(2)}, u32[]{:S(2)}) collective-permute-start(bf16[256,1024]{1,0:T(8,128)(2,1)S(1)} %collective-permute-done.6.refs_1_), channel_id=1, source_target_pairs={{0,4},{8,0},{16,8},{24,16},{28,24},{20,28},{12,20},{4,12},{1,5},{9... | collective-permute-start | bytes 1572872 | tf_op jit(solution)/shard_map/ppermute | solution.py:35
  79.0 3.0 %collective-permute-done.16.refs_1_ = bf16[256,1024]{1,0:T(8,128)(2,1)S(1)} collective-permute-done((bf16[256,1024]{1,0:T(8,128)(2,1)}, bf16[256,1024]{1,0:T(8,128)(2,1)S(1)}, u32[]{:S(2)}, u32[]{:S(2)}) %collective-permute-start.16) | collective-permute-done | bytes 524320 | tf_op jit(solution)/shard_map/ppermute | solution.py:35
  86.2 1.6 collective-permute-start.24
  88.6 4.1 %collective-permute-done.7.refs_1_ = bf16[256,1024]{1,0:T(8,128)(2,1)S(1)} collective-permute-done((bf16[256,1024]{1,0:T(8,128)(2,1)S(1)}, bf16[256,1024]{1,0:T(8,128)(2,1)S(1)}, u32[]{:S(2)}, u32[]{:S(2)}) %collective-permute-start.7) | collective-permute-done | bytes 524320 | tf_op jit(solution)/shard_map/ppermute | solution.py:35
  94.2 12.5 %collective-permute-done.27.refs_6_ = bf16[2,640,256]{2,1,0:T(8,128)(2,1)S(1)} collective-permute-done((bf16[2,640,256]{2,1,0:T(8,128)(2,1)S(1)}, bf16[2,640,256]{2,1,0:T(8,128)(2,1)S(1)}, u32[]{:S(2)}, u32[]{:S(2)}) %collective-permute-start.27) | collective-permute-done | bytes 655392 | tf_op jit(solution)/shard_map/ppermute | solution.py:93
  106.7 12.1 %collective-permute-done.24.refs_6_ = bf16[2,640,256]{2,1,0:T(8,128)(2,1)S(1)} collective-permute-done((bf16[2,640,256]{2,1,0:T(8,128)(2,1)S(1)}, bf16[2,640,256]{2,1,0:T(8,128)(2,1)S(1)}, u32[]{:S(2)}, u32[]{:S(2)}) %collective-permute-start.24) | collective-permute-done | bytes 655392 | tf_op jit(solution)/shard_map/ppermute | solution.py:93
  119.4 1.6 collective-permute-start.21
  122.8 1.6 collective-permute-start.9
  124.4 5.7 %collective-permute-done.21.refs_4_ = bf16[1,640,256]{2,1,0:T(8,128)(2,1)S(1)} collective-permute-done((bf16[1,640,256]{2,1,0:T(8,128)(2,1)S(1)}, bf16[1,640,256]{2,1,0:T(8,128)(2,1)S(1)}, u32[]{:S(2)}, u32[]{:S(2)}) %collective-permute-start.21) | collective-permute-done | bytes 327712 | tf_op jit(solution)/shard_map/ppermute | solution.py:93
  130.1 7.0 %collective-permute-done.18.refs_4_ = bf16[1,640,256]{2,1,0:T(8,128)(2,1)S(1)} collective-permute-done((bf16[1,640,256]{2,1,0:T(8,128)(2,1)S(1)}, bf16[1,640,256]{2,1,0:T(8,128)(2,1)S(1)}, u32[]{:S(2)}, u32[]{:S(2)}) %collective-permute-start.18) | collective-permute-done | bytes 327712 | tf_op jit(solution)/shard_map/ppermute | solution.py:93
  137.1 6.6 %collective-permute-done.9.refs_4_ = bf16[1,640,256]{2,1,0:T(8,128)(2,1)S(1)} collective-permute-done((bf16[1,640,256]{2,1,0:T(8,128)(2,1)S(1)}, bf16[1,640,256]{2,1,0:T(8,128)(2,1)S(1)}, u32[]{:S(2)}, u32[]{:S(2)}) %collective-permute-start.9) | collective-permute-done | bytes 327712 | tf_op jit(solution)/shard_map/ppermute | solution.py:93
  143.6 2.6 %shard_map.42 = (f32[640,1024]{1,0:T(8,128)S(1)}, f32[16,1024]{1,0:T(8,128)S(1)}, f32[2,640,128]{2,1,0:T(8,128)S(1)}) custom-call(s32[8]{0:T(128)S(1)} %stack.35.where, bf16[256,1024]{1,0:T(8,128)(2,1)S(1)} %get-tuple-element.37.refs_0_, bf16[256,1024]{1,0:T(8,128)(2,1)S(1)} %get-tuple-element.36.refs_1_, bf16[2,640,256]{2,1,0:T(8,128)(2,1)S(1)} %shard_map.40.mine.refs_2_, ...), custom_call_target="tpu_custom_call" | custom-call | tf_op jit(solution)/shard_map/pallas_call | solution.py:228
  146.2 4.7 %shard_map.43 = (f32[640,1024]{1,0:T(8,128)S(1)}, f32[16,1024]{1,0:T(8,128)S(1)}, f32[2,640,128]{2,1,0:T(8,128)S(1)}) custom-call(s32[8]{0:T(128)S(1)} %stack.35.where, bf16[256,1024]{1,0:T(8,128)(2,1)S(1)} %collective-permute-done.refs_0_, ...), custom_call_target="tpu_custom_call", output_to_operand_aliasing={{0}: (9, {}), {1}: (10, {}), {2}: (11, {})} | custom-call | tf_op jit(solution)/shard_map/pallas_call | solution.py:228
  150.9 5.0 %shard_map.44 = (f32[640,1024]{1,0:T(8,128)S(1)}, f32[16,1024]{1,0:T(8,128)S(1)}, f32[2,640,128]{2,1,0:T(8,128)S(1)}) custom-call(s32[8]{0:T(128)S(1)} %stack.35.where, bf16[256,1024]{1,0:T(8,128)(2,1)S(1)} %collective-permute-done.1.refs_0_, ...), custom_call_target="tpu_custom_call", output_to_operand_aliasing={{0}: (9, {}), {1}: (10, {}), {2}: (11, {})} | custom-call | tf_op jit(solution)/shard_map/pallas_call | solution.py:228
  155.9 2.8 %shard_map.45 = (f32[640,1024]{1,0:T(8,128)S(1)}, f32[16,1024]{1,0:T(8,128)S(1)}, f32[2,640,128]{2,1,0:T(8,128)S(1)}) custom-call(s32[8]{0:T(128)S(1)} %stack.35.where, bf16[256,1024]{1,0:T(8,128)(2,1)S(1)} %collective-permute-done.2.refs_0_, ...), custom_call_target="tpu_custom_call", output_to_operand_aliasing={{0}: (7, {}), {1}: (8, {}), {2}: (9, {})} | custom-call | tf_op jit(solution)/shard_map/pallas_call | solution.py:228
  158.7 2.8 %shard_map.46 = (f32[640,1024]{1,0:T(8,128)S(1)}, f32[16,1024]{1,0:T(8,128)S(1)}, f32[2,640,128]{2,1,0:T(8,128)S(1)}) custom-call(s32[8]{0:T(128)S(1)} %stack.35.where, bf16[256,1024]{1,0:T(8,128)(2,1)S(1)} %collective-permute-done.13.refs_0_, ...), custom_call_target="tpu_custom_call", output_to_operand_aliasing={{0}: (7, {}), {1}: (8, {}), {2}: (9, {})} | custom-call | tf_op jit(solution)/shard_map/pallas_call | solution.py:228
  161.5 3.9 %shard_map.47 = (f32[512,1024]{1,0:T(8,128)}, f32[128,1024]{1,0:T(8,128)}) custom-call(s32[8]{0:T(128)S(1)} %stack.35.where, bf16[256,1024]{1,0:T(8,128)(2,1)S(1)} %collective-permute-done.3.refs_0_, bf16[256,1024]{1,0:T(8,128)(2,1)S(1)} %collective-permute-done.7.refs_1_, bf16[2,640,256]{2,1,0:T(8,128)(2,1)S(1)} %shard_map.30.mine.refs_2_, ...), custom_call_target="tpu_custom_call" | custom-call | tf_op jit(solution)/shard_map/pallas_call | solution.py:228
  (52 shorter events, 18.6 us)
Async XLA Ops:
  1.9 15.8 %collective-permute-start = (bf16[256,1024]{1,0:T(8,128)(2,1)S(1)}, bf16[256,1024]{1,0:T(8,128)(2,1)S(1)}, u32[]{:S(2)}, u32[]{:S(2)}) collective-permute-start(bf16[256,1024]{1,0:T(8,128)(2,1)S(1)} %get-tuple-element.37.refs_0_), channel_id=1, source_target_pairs={{0,8},{8,16},{16,24},{24,28},{28,20},{20,12},{12,4},{4,0},{1,9},{9... | collective-permute-start | bytes 1572872 | tf_op jit(solution)/shard_map/ppermute | solution.py:34
  5.0 23.9 %collective-permute-start.11 = (bf16[256,1024]{1,0:T(8,128)(2,1)S(1)}, bf16[256,1024]{1,0:T(8,128)(2,1)S(1)}, u32[]{:S(2)}, u32[]{:S(2)}) collective-permute-start(bf16[256,1024]{1,0:T(8,128)(2,1)S(1)} %get-tuple-element.36.refs_1_), channel_id=1, source_target_pairs={{0,8},{8,16},{16,24},{24,28},{28,20},{20,12},{12,4},{4,0},{1,9},{9... | collective-permute-start | bytes 1572872 | tf_op jit(solution)/shard_map/ppermute | solution.py:34
  6.6 24.5 %collective-permute-start.14 = (bf16[256,1024]{1,0:T(8,128)(2,1)S(1)}, bf16[256,1024]{1,0:T(8,128)(2,1)S(1)}, u32[]{:S(2)}, u32[]{:S(2)}) collective-permute-start(bf16[256,1024]{1,0:T(8,128)(2,1)S(1)} %get-tuple-element.37.refs_0_), channel_id=1, source_target_pairs={{0,4},{8,0},{16,8},{24,16},{28,24},{20,28},{12,20},{4,12},{1,5},{9... | collective-permute-start | bytes 1572872 | tf_op jit(solution)/shard_map/ppermute | solution.py:35
  7.0 24.0 %collective-permute-start.4 = (bf16[256,1024]{1,0:T(8,128)(2,1)S(1)}, bf16[256,1024]{1,0:T(8,128)(2,1)}, u32[]{:S(2)}, u32[]{:S(2)}) collective-permute-start(bf16[256,1024]{1,0:T(8,128)(2,1)S(1)} %get-tuple-element.36.refs_1_), channel_id=1, source_target_pairs={{0,4},{8,0},{16,8},{24,16},{28,24},{20,28},{12,20},{4,12},{1,5},{9... | collective-permute-start | bytes 1572872 | tf_op jit(solution)/shard_map/ppermute | solution.py:35
  17.7 22.5 %collective-permute-start.1 = (bf16[256,1024]{1,0:T(8,128)(2,1)S(1)}, bf16[256,1024]{1,0:T(8,128)(2,1)S(1)}, u32[]{:S(2)}, u32[]{:S(2)}) collective-permute-start(bf16[256,1024]{1,0:T(8,128)(2,1)S(1)} %collective-permute-done.refs_0_), channel_id=1, source_target_pairs={{0,8},{8,16},{16,24},{24,28},{28,20},{20,12},{12,4},{4,0},{1,9},{9... | collective-permute-start | bytes 1572872 | tf_op jit(solution)/shard_map/ppermute | solution.py:34
  28.9 21.7 %collective-permute-start.12 = (bf16[256,1024]{1,0:T(8,128)(2,1)S(1)}, bf16[256,1024]{1,0:T(8,128)(2,1)}, u32[]{:S(2)}, u32[]{:S(2)}) collective-permute-start(bf16[256,1024]{1,0:T(8,128)(2,1)S(1)} %collective-permute-done.11.refs_2_), channel_id=1, source_target_pairs={{0,8},{8,16},{16,24},{24,28},{28,20},{20,12},{12,4},{4,0},{1,9},{9... | collective-permute-start | bytes 1572872 | tf_op jit(solution)/shard_map/ppermute | solution.py:34
  31.0 21.4 %collective-permute-start.15 = (bf16[256,1024]{1,0:T(8,128)(2,1)S(1)}, bf16[256,1024]{1,0:T(8,128)(2,1)}, u32[]{:S(2)}, u32[]{:S(2)}) collective-permute-start(bf16[256,1024]{1,0:T(8,128)(2,1)S(1)} %collective-permute-done.14.refs_3_), channel_id=1, source_target_pairs={{0,4},{8,0},{16,8},{24,16},{28,24},{20,28},{12,20},{4,12},{1,5},{9... | collective-permute-start | bytes 1572872 | tf_op jit(solution)/shard_map/ppermute | solution.py:35
  31.1 22.8 %collective-permute-start.5 = (bf16[256,1024]{1,0:T(8,128)(2,1)}, bf16[256,1024]{1,0:T(8,128)(2,1)}, u32[]{:S(2)}, u32[]{:S(2)}) collective-permute-start(bf16[256,1024]{1,0:T(8,128)(2,1)} %collective-permute-done.4.refs_1_), channel_id=1, source_target_pairs={{0,4},{8,0},{16,8},{24,16},{28,24},{20,28},{12,20},{4,12},{1,5},{9... | collective-permute-start | bytes 1572872 | tf_op jit(solution)/shard_map/ppermute | solution.py:35
  33.8 22.4 %collective-permute-start.29 = (bf16[2,640,256]{2,1,0:T(8,128)(2,1)S(1)}, bf16[2,640,256]{2,1,0:T(8,128)(2,1)S(1)}, u32[]{:S(2)}, u32[]{:S(2)}) collective-permute-start(bf16[2,640,256]{2,1,0:T(8,128)(2,1)S(1)} %shard_map.40.mine.refs_2_), channel_id=1, source_target_pairs={{0,1},{1,0},{2,3},{3,2},{4,5},{5,4},{6,7},{7,6},{8,9},{9,8},{10,11... | collective-permute-start | bytes 1966088 | tf_op jit(solution)/shard_map/ppermute | solution.py:90
  40.2 44.1 %collective-permute-start.26 = (bf16[4,640,256]{2,1,0:T(8,128)(2,1)S(1)}, bf16[4,640,256]{2,1,0:T(8,128)(2,1)S(1)}, u32[]{:S(2)}, u32[]{:S(2)}) collective-permute-start(bf16[4,640,256]{2,1,0:T(8,128)(2,1)S(1)} %shard_map.38.mine.refs_4_), channel_id=1, source_target_pairs={{0,1},{1,0},{2,3},{3,2},{4,5},{5,4},{6,7},{7,6},{8,9},{9,8},{10,11... | collective-permute-start | bytes 3932168 | tf_op jit(solution)/shard_map/ppermute | solution.py:90
  50.7 14.8 %collective-permute-start.2 = (bf16[256,1024]{1,0:T(8,128)(2,1)S(1)}, bf16[256,1024]{1,0:T(8,128)(2,1)S(1)}, u32[]{:S(2)}, u32[]{:S(2)}) collective-permute-start(bf16[256,1024]{1,0:T(8,128)(2,1)S(1)} %collective-permute-done.1.refs_0_), channel_id=1, source_target_pairs={{0,8},{8,16},{16,24},{24,28},{28,20},{20,12},{12,4},{4,0},{1,9},{9... | collective-permute-start | bytes 1572872 | tf_op jit(solution)/shard_map/ppermute | solution.py:34
  55.7 29.4 %collective-permute-start.23 = (bf16[4,640,256]{2,1,0:T(8,128)(2,1)S(1)}, bf16[4,640,256]{2,1,0:T(8,128)(2,1)S(1)}, u32[]{:S(2)}, u32[]{:S(2)}) collective-permute-start(bf16[4,640,256]{2,1,0:T(8,128)(2,1)S(1)} %shard_map.36.mine.refs_4_), channel_id=1, source_target_pairs={{0,1},{1,0},{2,3},{3,2},{4,5},{5,4},{6,7},{7,6},{8,9},{9,8},{10,11... | collective-permute-start | bytes 3932168 | tf_op jit(solution)/shard_map/ppermute | solution.py:90
  55.7 15.1 %collective-permute-start.6 = (bf16[256,1024]{1,0:T(8,128)(2,1)}, bf16[256,1024]{1,0:T(8,128)(2,1)S(1)}, u32[]{:S(2)}, u32[]{:S(2)}) collective-permute-start(bf16[256,1024]{1,0:T(8,128)(2,1)} %collective-permute-done.5.refs_1_), channel_id=1, source_target_pairs={{0,4},{8,0},{16,8},{24,16},{28,24},{20,28},{12,20},{4,12},{1,5},{9... | collective-permute-start | bytes 1572872 | tf_op jit(solution)/shard_map/ppermute | solution.py:35
  56.3 20.4 %collective-permute-start.13 = (bf16[256,1024]{1,0:T(8,128)(2,1)}, bf16[256,1024]{1,0:T(8,128)(2,1)S(1)}, u32[]{:S(2)}, u32[]{:S(2)}) collective-permute-start(bf16[256,1024]{1,0:T(8,128)(2,1)} %collective-permute-done.12.refs_2_), channel_id=1, source_target_pairs={{0,8},{8,16},{16,24},{24,28},{28,20},{20,12},{12,4},{4,0},{1,9},{9... | collective-permute-start | bytes 1572872 | tf_op jit(solution)/shard_map/ppermute | solution.py:34
  65.5 16.6 %collective-permute-start.16 = (bf16[256,1024]{1,0:T(8,128)(2,1)}, bf16[256,1024]{1,0:T(8,128)(2,1)S(1)}, u32[]{:S(2)}, u32[]{:S(2)}) collective-permute-start(bf16[256,1024]{1,0:T(8,128)(2,1)} %collective-permute-done.15.refs_3_), channel_id=1, source_target_pairs={{0,4},{8,0},{16,8},{24,16},{28,24},{20,28},{12,20},{4,12},{1,5},{9... | collective-permute-start | bytes 1572872 | tf_op jit(solution)/shard_map/ppermute | solution.py:35
  70.8 15.4 %collective-permute-start.3 = (bf16[256,1024]{1,0:T(8,128)(2,1)S(1)}, bf16[256,1024]{1,0:T(8,128)(2,1)S(1)}, u32[]{:S(2)}, u32[]{:S(2)}) collective-permute-start(bf16[256,1024]{1,0:T(8,128)(2,1)S(1)} %collective-permute-done.2.refs_0_), channel_id=1, source_target_pairs={{0,8},{8,16},{16,24},{24,28},{28,20},{20,12},{12,4},{4,0},{1,9},{9... | collective-permute-start | bytes 1572872 | tf_op jit(solution)/shard_map/ppermute | solution.py:34
  76.7 16.0 %collective-permute-start.7 = (bf16[256,1024]{1,0:T(8,128)(2,1)S(1)}, bf16[256,1024]{1,0:T(8,128)(2,1)S(1)}, u32[]{:S(2)}, u32[]{:S(2)}) collective-permute-start(bf16[256,1024]{1,0:T(8,128)(2,1)S(1)} %collective-permute-done.6.refs_1_), channel_id=1, source_target_pairs={{0,4},{8,0},{16,8},{24,16},{28,24},{20,28},{12,20},{4,12},{1,5},{9... | collective-permute-start | bytes 1572872 | tf_op jit(solution)/shard_map/ppermute | solution.py:35
  82.0 11.5 %collective-permute-start.30 = (bf16[1,640,256]{2,1,0:T(8,128)(2,1)S(1)}, bf16[1,640,256]{2,1,0:T(8,128)(2,1)S(1)}, u32[]{:S(2)}, u32[]{:S(2)}) collective-permute-start(bf16[1,640,256]{2,1,0:T(8,128)(2,1)S(1)} %shard_map.41), channel_id=1, source_target_pairs={{0,2},{1,3},{2,0},{3,1},{4,6},{5,7},{6,4},{7,5},{8,10},{9,11},{10,... | collective-permute-start | bytes 983048 | tf_op jit(solution)/shard_map/ppermute | solution.py:93
  84.3 9.8 %collective-permute-start.20 = (bf16[2,640,256]{2,1,0:T(8,128)(2,1)S(1)}, bf16[2,640,256]{2,1,0:T(8,128)(2,1)S(1)}, u32[]{:S(2)}, u32[]{:S(2)}) collective-permute-start(bf16[2,640,256]{2,1,0:T(8,128)(2,1)S(1)} %shard_map.34.mine.refs_2_), channel_id=1, source_target_pairs={{0,1},{1,0},{2,3},{3,2},{4,5},{5,4},{6,7},{7,6},{8,9},{9,8},{10,11... | collective-permute-start | bytes 1966088 | tf_op jit(solution)/shard_map/ppermute | solution.py:90
  85.0 21.6 %collective-permute-start.27 = (bf16[2,640,256]{2,1,0:T(8,128)(2,1)S(1)}, bf16[2,640,256]{2,1,0:T(8,128)(2,1)S(1)}, u32[]{:S(2)}, u32[]{:S(2)}) collective-permute-start(bf16[2,640,256]{2,1,0:T(8,128)(2,1)S(1)} %shard_map.39), channel_id=1, source_target_pairs={{0,2},{1,3},{2,0},{3,1},{4,6},{5,7},{6,4},{7,5},{8,10},{9,11},{10,... | collective-permute-start | bytes 1966088 | tf_op jit(solution)/shard_map/ppermute | solution.py:93
  86.2 32.6 %collective-permute-start.24 = (bf16[2,640,256]{2,1,0:T(8,128)(2,1)S(1)}, bf16[2,640,256]{2,1,0:T(8,128)(2,1)S(1)}, u32[]{:S(2)}, u32[]{:S(2)}) collective-permute-start(bf16[2,640,256]{2,1,0:T(8,128)(2,1)S(1)} %shard_map.37), channel_id=1, source_target_pairs={{0,2},{1,3},{2,0},{3,1},{4,6},{5,7},{6,4},{7,5},{8,10},{9,11},{10,... | collective-permute-start | bytes 1966088 | tf_op jit(solution)/shard_map/ppermute | solution.py:93
  92.7 26.7 %collective-permute-start.17 = (bf16[2,640,256]{2,1,0:T(8,128)(2,1)S(1)}, bf16[2,640,256]{2,1,0:T(8,128)(2,1)S(1)}, u32[]{:S(2)}, u32[]{:S(2)}) collective-permute-start(bf16[2,640,256]{2,1,0:T(8,128)(2,1)S(1)} %shard_map.32.mine.refs_2_), channel_id=1, source_target_pairs={{0,1},{1,0},{2,3},{3,2},{4,5},{5,4},{6,7},{7,6},{8,9},{9,8},{10,11... | collective-permute-start | bytes 1966088 | tf_op jit(solution)/shard_map/ppermute | solution.py:90
  93.5 28.1 %collective-permute-start.8 = (bf16[2,640,256]{2,1,0:T(8,128)(2,1)S(1)}, bf16[2,640,256]{2,1,0:T(8,128)(2,1)S(1)}, u32[]{:S(2)}, u32[]{:S(2)}) collective-permute-start(bf16[2,640,256]{2,1,0:T(8,128)(2,1)S(1)} %shard_map.30.mine.refs_2_), channel_id=1, source_target_pairs={{0,1},{1,0},{2,3},{3,2},{4,5},{5,4},{6,7},{7,6},{8,9},{9,8},{10,11... | collective-permute-start | bytes 1966088 | tf_op jit(solution)/shard_map/ppermute | solution.py:90
  94.1 28.7 %collective-permute-start.31 = (bf16[1,640,256]{2,1,0:T(8,128)(2,1)S(1)}, bf16[1,640,256]{2,1,0:T(8,128)(2,1)S(1)}, u32[]{:S(2)}, u32[]{:S(2)}) collective-permute-start(bf16[1,640,256]{2,1,0:T(8,128)(2,1)S(1)} %collective-permute-done.30.refs_4_), channel_id=1, source_target_pairs={{0,1},{1,0},{2,3},{3,2},{4,5},{5,4},{6,7},{7,6},{8,9},{9,8},{10,11... | collective-permute-start | bytes 983048 | tf_op jit(solution)/shard_map/ppermute | solution.py:94
  106.6 39.6 %collective-permute-start.28 = (bf16[2,640,256]{2,1,0:T(8,128)(2,1)S(1)}, bf16[2,640,256]{2,1,0:T(8,128)(2,1)S(1)}, u32[]{:S(2)}, u32[]{:S(2)}) collective-permute-start(bf16[2,640,256]{2,1,0:T(8,128)(2,1)S(1)} %collective-permute-done.27.refs_6_), channel_id=1, source_target_pairs={{0,1},{1,0},{2,3},{3,2},{4,5},{5,4},{6,7},{7,6},{8,9},{9,8},{10,11... | collective-permute-start | bytes 1966088 | tf_op jit(solution)/shard_map/ppermute | solution.py:94
  118.8 32.1 %collective-permute-start.25 = (bf16[2,640,256]{2,1,0:T(8,128)(2,1)S(1)}, bf16[2,640,256]{2,1,0:T(8,128)(2,1)S(1)}, u32[]{:S(2)}, u32[]{:S(2)}) collective-permute-start(bf16[2,640,256]{2,1,0:T(8,128)(2,1)S(1)} %collective-permute-done.24.refs_6_), channel_id=1, source_target_pairs={{0,1},{1,0},{2,3},{3,2},{4,5},{5,4},{6,7},{7,6},{8,9},{9,8},{10,11... | collective-permute-start | bytes 1966088 | tf_op jit(solution)/shard_map/ppermute | solution.py:94
  119.4 10.6 %collective-permute-start.21 = (bf16[1,640,256]{2,1,0:T(8,128)(2,1)S(1)}, bf16[1,640,256]{2,1,0:T(8,128)(2,1)S(1)}, u32[]{:S(2)}, u32[]{:S(2)}) collective-permute-start(bf16[1,640,256]{2,1,0:T(8,128)(2,1)S(1)} %shard_map.35), channel_id=1, source_target_pairs={{0,2},{1,3},{2,0},{3,1},{4,6},{5,7},{6,4},{7,5},{8,10},{9,11},{10,... | collective-permute-start | bytes 983048 | tf_op jit(solution)/shard_map/ppermute | solution.py:93
  121.6 15.5 %collective-permute-start.18 = (bf16[1,640,256]{2,1,0:T(8,128)(2,1)S(1)}, bf16[1,640,256]{2,1,0:T(8,128)(2,1)S(1)}, u32[]{:S(2)}, u32[]{:S(2)}) collective-permute-start(bf16[1,640,256]{2,1,0:T(8,128)(2,1)S(1)} %shard_map.33), channel_id=1, source_target_pairs={{0,2},{1,3},{2,0},{3,1},{4,6},{5,7},{6,4},{7,5},{8,10},{9,11},{10,... | collective-permute-start | bytes 983048 | tf_op jit(solution)/shard_map/ppermute | solution.py:93
  122.8 20.9 %collective-permute-start.9 = (bf16[1,640,256]{2,1,0:T(8,128)(2,1)S(1)}, bf16[1,640,256]{2,1,0:T(8,128)(2,1)S(1)}, u32[]{:S(2)}, u32[]{:S(2)}) collective-permute-start(bf16[1,640,256]{2,1,0:T(8,128)(2,1)S(1)} %shard_map.31), channel_id=1, source_target_pairs={{0,2},{1,3},{2,0},{3,1},{4,6},{5,7},{6,4},{7,5},{8,10},{9,11},{10,... | collective-permute-start | bytes 983048 | tf_op jit(solution)/shard_map/ppermute | solution.py:93
  130.1 25.8 %collective-permute-start.22 = (bf16[1,640,256]{2,1,0:T(8,128)(2,1)S(1)}, bf16[1,640,256]{2,1,0:T(8,128)(2,1)S(1)}, u32[]{:S(2)}, u32[]{:S(2)}) collective-permute-start(bf16[1,640,256]{2,1,0:T(8,128)(2,1)S(1)} %collective-permute-done.21.refs_4_), channel_id=1, source_target_pairs={{0,1},{1,0},{2,3},{3,2},{4,5},{5,4},{6,7},{7,6},{8,9},{9,8},{10,11... | collective-permute-start | bytes 983048 | tf_op jit(solution)/shard_map/ppermute | solution.py:94
  137.1 21.6 %collective-permute-start.19 = (bf16[1,640,256]{2,1,0:T(8,128)(2,1)S(1)}, bf16[1,640,256]{2,1,0:T(8,128)(2,1)S(1)}, u32[]{:S(2)}, u32[]{:S(2)}) collective-permute-start(bf16[1,640,256]{2,1,0:T(8,128)(2,1)S(1)} %collective-permute-done.18.refs_4_), channel_id=1, source_target_pairs={{0,1},{1,0},{2,3},{3,2},{4,5},{5,4},{6,7},{7,6},{8,9},{9,8},{10,11... | collective-permute-start | bytes 983048 | tf_op jit(solution)/shard_map/ppermute | solution.py:94
  143.6 17.9 %collective-permute-start.10 = (bf16[1,640,256]{2,1,0:T(8,128)(2,1)S(1)}, bf16[1,640,256]{2,1,0:T(8,128)(2,1)S(1)}, u32[]{:S(2)}, u32[]{:S(2)}) collective-permute-start(bf16[1,640,256]{2,1,0:T(8,128)(2,1)S(1)} %collective-permute-done.9.refs_4_), channel_id=1, source_target_pairs={{0,1},{1,0},{2,3},{3,2},{4,5},{5,4},{6,7},{7,6},{8,9},{9,8},{10,11... | collective-permute-start | bytes 983048 | tf_op jit(solution)/shard_map/ppermute | solution.py:94

commit v2 on v1

v2 whole, which is shorter than its diff:
```python
import functools

import jax
import jax.numpy as jnp
from jax import lax
from jax.experimental import pallas as pl
from jax.experimental.pallas import tpu as pltpu
from jax.sharding import PartitionSpec as P


OV = 1024


var_floor = 0.05


def ring_pairs(size, step):
    order = list(range(0, size, 2)) + list(range(1, size, 2))[::-1]
    return [(order[i], order[(i + step) % size]) for i in range(size)]


def ring_chunks(own):
    size = lax.axis_size("samp")
    half = own.shape[0] // 2
    ahead = ring_pairs(size, 1)
    back = ring_pairs(size, -1)
    fore = [own[:half], own[half:]]
    aft = [own[half:], own[:half]]
    groups = [[own[:half], own[half:]]]
    for step in range(size - 1):
        lane = step % 2
        fore[lane] = lax.ppermute(fore[lane], "samp", ahead)
        aft[lane] = lax.ppermute(aft[lane], "samp", back)
        groups.append([fore[lane], aft[lane]])
    return groups


def parts_of(where, width, win_cols, base=0):
    return (
        (where[base + 2], where[base + 3], slice(0, win_cols)),
        (where[base + 4], where[base + 5], slice(win_cols, width)),
    )


def pick_columns(where, *refs, win_cols):
    count = (len(where) - 8) // 16
    chunks, outs = refs[: len(refs) - 1 - count], refs[len(refs) - 1 - count :]
    for i, chunk in enumerate(chunks):
        for out, base in zip(outs, (0, 8 + 8 * (i % 2))):
            parts = parts_of(where, out.shape[1], win_cols)
            for at, (_, _, part) in zip((where[base], where[base + 1]), parts):
                at = pl.ds(pl.multiple_of(at, 128), part.stop - part.start)
                out[i, part] = chunk[:, at].T


def pick_core(where, *refs, win_cols):
    outs = refs[len(refs) * 2 // 3 :]
    for i, out in enumerate(outs):
        mine, theirs = refs[2 * i : 2 * i + 2]
        half = out.shape[0]
        start = where[6] * half
        base = 0 if i == 0 else 8 + 8 * where[6]
        for core, _, part in parts_of(where, out.shape[1], win_cols, base):

            @pl.when(core == where[6])
            def _():
                out[:, part] = mine[pl.ds(start, half), part]

            @pl.when(core != where[6])
            def _():
                out[:, part] = theirs[pl.ds(start, half), part]


def local_call(body, shapes, operands, win_cols):
    vmem = pl.BlockSpec(memory_space=pltpu.VMEM)
    smem = pl.BlockSpec(memory_space=pltpu.SMEM)
    return pl.pallas_call(
        functools.partial(body, win_cols=win_cols),
        out_shape=[jax.ShapeDtypeStruct(shape, jnp.bfloat16) for shape in shapes],
        in_specs=[smem] + [vmem] * (len(operands) - 1),
        out_specs=[vmem] * len(shapes),
        compiler_params=pltpu.CompilerParams(vmem_limit_bytes=8 << 20),
    )(*operands)


def wanted_rows(groups, where, after, win_cols, band_cols):
    swap = [(0, 1), (1, 0), (2, 3), (3, 2)]
    across = [(0, 2), (1, 3), (2, 0), (3, 1)]
    size = lax.axis_size("samp")
    onward = [
        (4 * a + 2 * pair + core, 4 * b + 2 * pair + core)
        for core, step in ((0, 1), (1, -1))
        for a, b in ring_pairs(size, step)
        for pair in (0, 1)
    ]
    final = len(groups) - 1
    pieces = []
    early = None
    for index, group in enumerate(groups):
        shape = (len(group), win_cols + band_cols, group[0].shape[0])
        half = (len(group) // 2,) + shape[1:]
        ahead = index == final - 2
        at = after if ahead else where
        count = 2 if ahead else 1
        mine = local_call(pick_columns, [shape] * count, (at, *group), win_cols)
        theirs = [lax.ppermute(mine[0], "snp", swap)]
        if index == final:
            came = early
        else:
            if ahead:
                theirs.append(lax.ppermute(mine[1], "snp", swap))
            held = [piece for both in zip(mine, theirs) for piece in both]
            sent = local_call(pick_core, [half] * count, (at, *held), win_cols)
            if ahead:
                early = lax.ppermute(sent[1], "snp", across)
                early = lax.ppermute(early, ("samp", "snp"), onward)
            came = lax.ppermute(sent[0], "snp", across)
        other = lax.ppermute(came, "snp", swap)
        pieces.append((mine[0], theirs[0], came, other))
    return pieces


def gather_rows(where, pieces, slab, win_cols):
    mine, theirs, came, other = pieces
    size, row_width, rows = mine.shape

    def fill(part, places):
        for i, (piece, j) in enumerate(places):
            slab[part, i * rows : i * rows + rows] = piece[j, part]

    def pair_of(first, second):
        half = size // 2
        return [(first, j) for j in range(half)] + [(second, j) for j in range(half)]

    for core, pair, part in parts_of(where, row_width, win_cols):
        near = pair == where[7]
        far = jnp.logical_not(near)

        @pl.when(near & (core == where[6]))
        def _():
            fill(part, [(mine, j) for j in range(size)])

        @pl.when(near & (core != where[6]))
        def _():
            fill(part, [(theirs, j) for j in range(size)])

        @pl.when(far & (where[6] == 0))
        def _():
            fill(part, pair_of(came, other))

        @pl.when(far & (where[6] == 1))
        def _():
            fill(part, pair_of(other, came))


def add_stats(groups, slabs, col_before, row_before, col_out, row_out):
    for out, op in ((0, lambda v: v), (1, lambda v: v * v)):
        at = slice(8 * out, 8 * out + 8)
        total = None if col_before is None else col_before[at]
        for col in [col for cols in groups for col in cols]:
            wide = op(col[...].astype(jnp.float32))
            part = jnp.sum(wide.reshape(-1, 8, wide.shape[1]), axis=0)
            total = part if total is None else total + part
        col_out[at] = total
        total = None if row_before is None else row_before[out]
        for slab in slabs:
            for j in range(0, slab.shape[1], 128):
                part = op(slab[:, j : j + 128].astype(jnp.float32))
                total = part if total is None else total + part
        row_out[out] = total


def add_sums(groups, slabs, at, before):
    total = before
    for cols, slab in zip(groups, slabs):
        col = jnp.concatenate([col[:, at] for col in cols], axis=0)
        part = jnp.dot(slab[...], col, preferred_element_type=jnp.float32)
        total = part if total is None else total + part
    return total


def split_refs(refs, sizes):
    groups, pieces, start = [], [], 0
    for size in sizes:
        groups.append(refs[start : start + size])
        pieces.append(refs[start + size : start + size + 4])
        start += size + 4
    return groups, pieces, refs[start:]


def first_sums(where, *refs, sizes, first, win_cols):
    groups, pieces, refs = split_refs(refs, sizes)
    before = (None, None, None) if first else refs[:3]
    gram, col_out, row_out = refs[-3 - len(sizes) : -len(sizes)]
    slabs = refs[-len(sizes) :]
    for piece, slab in zip(pieces, slabs):
        gather_rows(where, piece, slab, win_cols)
    add_stats(groups, slabs, before[1], before[2], col_out, row_out)
    tile = 256

    def columns(j, carry):
        at = pl.ds(pl.multiple_of(j * tile, tile), tile)
        gram[:, at] = add_sums(groups, slabs, at, None if first else before[0][:, at])
        return carry

    lax.fori_loop(0, gram.shape[1] // tile, columns, 0)


def last_sums(where, *refs, sizes, count, win_cols):
    groups, pieces, refs = split_refs(refs, sizes)
    before, (win_out, band_out) = refs[:3], refs[3:5]
    slabs, (col_stats, row_stats) = refs[5:-2], refs[-2:]
    step = pl.program_id(0)

    def moments(total, square, axis):
        mean = jnp.sum(total, axis=axis, keepdims=True) / count
        square = jnp.sum(square, axis=axis, keepdims=True) / count
        return mean, 1.0 / jnp.maximum(square - mean * mean, var_floor)

    @pl.when(step == 0)
    def _():
        for piece, slab in zip(pieces, slabs):
            gather_rows(where, piece, slab, win_cols)
        add_stats(groups, slabs, before[1], before[2], col_stats, row_stats)
        mean, inverse = moments(row_stats[0], row_stats[1], 1)
        row_stats[0] = jnp.broadcast_to(mean, row_stats.shape[1:])
        row_stats[1] = jnp.broadcast_to(inverse, row_stats.shape[1:])
        mean, inverse = moments(col_stats[0:8], col_stats[8:16], 0)
        col_stats[0:1] = mean
        col_stats[1:2] = inverse

    tile = win_out.shape[1]
    at = pl.ds(pl.multiple_of(step * tile, tile), tile)
    total = add_sums(groups, slabs, at, before[0][:, at])
    col_mean, col_inv = col_stats[0:1, at], col_stats[1:2, at]
    for j in range(0, tile, 128):
        part = slice(j, j + 128)
        covar = total[:, part] * (1.0 / count) - row_stats[0] * col_mean[:, part]
        ratio = covar * covar * (row_stats[1] * col_inv[:, part])
        win_out[:, part] = ratio[:win_cols]
        band_out[:, part] = ratio[win_cols:]


def summed(where, groups, rows, before, last, count, win_cols):
    width = groups[0][0].shape[1]
    row_width = rows[0][0].shape[1]
    operands = [where]
    for group, row in zip(groups, rows):
        operands += [*group, *row]
    operands += [] if before is None else list(before)
    sizes = tuple(len(group) for group in groups)
    gram = (row_width, width)
    sums = [gram, (16, width), (2, row_width, 128)]
    depth = groups[0][0].shape[0]
    slabs = [pltpu.VMEM((row_width, size * depth), jnp.bfloat16) for size in sizes]
    vmem = pl.BlockSpec(memory_space=pltpu.VMEM)
    smem = pl.BlockSpec(memory_space=pltpu.SMEM)
    if last:
        tile = 512
        body = functools.partial(last_sums, sizes=sizes, count=count, win_cols=win_cols)
        shapes = [(win_cols, width), (row_width - win_cols, width)]
        layout = dict(
            grid=(width // tile,),
            out_specs=[pl.BlockSpec((s[0], tile), lambda j: (0, j)) for s in shapes],
            scratch_shapes=slabs + [pltpu.VMEM(s, jnp.float32) for s in sums[1:]],
        )
    else:
        first = before is None
        body = functools.partial(first_sums, sizes=sizes, first=first, win_cols=win_cols)
        shapes = sums
        given = len(operands) - 3
        layout = dict(
            out_specs=[vmem] * 3,
            scratch_shapes=slabs,
            input_output_aliases={} if first else {given + i: i for i in range(3)},
        )
    return pl.pallas_call(
        body,
        out_shape=[jax.ShapeDtypeStruct(s, jnp.float32) for s in shapes],
        in_specs=[smem] + [vmem] * (len(operands) - 1),
        compiler_params=pltpu.CompilerParams(vmem_limit_bytes=16 << 20),
        **layout,
    )(*operands)


def shards(dosages):
    shard_count = lax.axis_size("samp")
    count = float(dosages.shape[0] * shard_count)
    width = dosages.shape[1]
    win_cols = width * lax.axis_size("snp") // shard_count
    band_cols = OV // shard_count
    samp, block = lax.axis_index("samp"), lax.axis_index("snp")

    def place(samp):
        row_at, band_at = samp * win_cols, samp * band_cols
        row_block, band_block = row_at // width, band_at // width
        return jnp.stack(
            [row_at % width, band_at % width, row_block % 2, row_block // 2]
            + [band_block % 2, band_block // 2, block % 2, block // 2]
        ).astype(jnp.int32)

    odd, end = samp % 2 == 1, shard_count - 2
    ahead = jnp.where(odd, jnp.maximum(samp - 2, 0), jnp.where(samp == end, end + 1, samp + 2))
    back = jnp.where(odd, jnp.where(samp > end, end, samp + 2), jnp.where(samp == 0, 1, samp - 2))
    where = place(samp)
    after = jnp.concatenate((where, place(ahead), place(back)))
    groups = ring_chunks(dosages)
    *groups[0], where, after = lax.optimization_barrier((*groups[0], where, after))
    rows = wanted_rows(groups, where, after, win_cols, band_cols)
    cuts = [0, 1, 2, 3, 4, 5, len(groups) - 2, len(groups)]
    total = None
    for start, stop in zip(cuts, cuts[1:]):
        part = slice(start, stop)
        last = stop == len(groups)
        total = summed(where, groups[part], rows[part], total, last, count, win_cols)
    return (total[0][None], total[1][None])


def passed_along(shard, axis, by):
    devices = lax.axis_size(axis)
    return lax.ppermute(shard, axis, [(i, (i + by) % devices) for i in range(devices)])


def squared_corr(gram, col_sum, col_sq, row_sum, row_sq, count):
    col_mean = col_sum / count
    row_mean = row_sum / count
    col_var = jnp.maximum(col_sq / count - col_mean * col_mean, var_floor)
    row_var = jnp.maximum(row_sq / count - row_mean * row_mean, var_floor)
    covar = gram / count - col_mean[:, None] * row_mean[None, :]
    return covar * covar / (col_var[:, None] * row_var[None, :])


def column_stats(block):
    return (
        jnp.sum(block, axis=0, dtype=jnp.float32),
        jnp.sum(jnp.square(block.astype(jnp.float32)), axis=0),
    )


def pair_sums(columns, own_rows):
    return lax.dot_general(
        columns, own_rows, (((0,), (0,)), ((), ())), preferred_element_type=jnp.float32
    )


def shards_by_sums(dosages):
    samples_here = dosages.shape[0]
    block_width = dosages.shape[1]
    shard_count = lax.axis_size("samp")
    count = jnp.float32(samples_here * shard_count)
    whole = lax.all_gather(dosages, "snp", axis=1, tiled=True)
    window_width = whole.shape[1]
    band = passed_along(whole[:, :OV], "win", -1)
    own_sum, own_sq = column_stats(dosages)
    total_sum, total_sq = lax.psum((own_sum, own_sq), "samp")
    win_sum, win_sq = (
        lax.all_gather(total_sum, "snp", axis=0, tiled=True),
        lax.all_gather(total_sq, "snp", axis=0, tiled=True),
    )
    next_sum, next_sq = passed_along((win_sum[:OV], win_sq[:OV]), "win", -1)
    win_cols = window_width // shard_count
    band_cols = OV // shard_count
    merged = jnp.concatenate(
        (
            whole.reshape(samples_here, shard_count, win_cols),
            band.reshape(samples_here, shard_count, band_cols),
        ),
        axis=2,
    ).reshape(samples_here, shard_count * (win_cols + band_cols))
    summed = lax.psum_scatter(pair_sums(merged, dosages), "samp", scatter_dimension=0, tiled=True)
    win_gram = summed[:win_cols]
    band_gram = summed[win_cols:]
    col_index = lax.axis_index("samp")
    row_index = lax.axis_index("snp")
    row_sum = lax.dynamic_slice_in_dim(win_sum, row_index * block_width, block_width, 0)
    row_sq = lax.dynamic_slice_in_dim(win_sq, row_index * block_width, block_width, 0)
    col_sum = lax.dynamic_slice_in_dim(win_sum, col_index * win_cols, win_cols, 0)
    col_sq = lax.dynamic_slice_in_dim(win_sq, col_index * win_cols, win_cols, 0)
    band_sum = lax.dynamic_slice_in_dim(next_sum, col_index * band_cols, band_cols, 0)
    band_sq = lax.dynamic_slice_in_dim(next_sq, col_index * band_cols, band_cols, 0)
    whole_out = squared_corr(win_gram, col_sum, col_sq, row_sum, row_sq, count)
    band_out = squared_corr(band_gram, band_sum, band_sq, row_sum, row_sq, count)
    return (whole_out[None], band_out[None])


def solution(mesh):
    near = mesh.shape["snp"] == 4 and mesh.shape["win"] == 1 and mesh.shape["samp"] == 8
    return jax.shard_map(
        shards if near else shards_by_sums,
        mesh=mesh,
        in_specs=(P("samp", ("win", "snp")),),
        out_specs=(P("win", "samp", "snp"), P("win", "samp", "snp")),
        check_vma=False,
    )
```

time: 166 us -> 148 us (0.89)
  waiting for transfers between devices: 103 us -> 77.7 us
  starting transfers between devices: 28.6 us -> 35.6 us
    ppermute x12 -> x18, waiting for transfers between devices: 43.9 us -> 27.6 us  [the longest x7 22.3 us: wanted_rows(): came = lax.ppermute(sent[0], 'snp', across)]
    ppermute x12 -> x18, starting transfers between devices: 8.21 us -> 15 us  [the longest x7 10.7 us: wanted_rows(): came = lax.ppermute(sent[0], 'snp', across)]
    ppermute x7, waiting for transfers between devices: 12.1 us -> 5.51 us  [ring_chunks(): aft[lane] = lax.ppermute(aft[lane], 'samp', back)]
    ppermute x7, starting transfers between devices: 13.8 us -> 11.4 us  [ring_chunks(): fore[lane] = lax.ppermute(fore[lane], 'samp', ahead)]
    ppermute x7, waiting for transfers between devices: 47 us -> 44.6 us  [ring_chunks(): fore[lane] = lax.ppermute(fore[lane], 'samp', ahead)]
    pallas_call x12 -> x15, Pallas kernels: 9.83 us -> 10.5 us  [local_call(): pl.pallas_call(functools.partial(body, win_cols=win_cols), out_shape=[jax...]
    pallas_call x6 -> x7, Pallas kernels: 21.7 us -> 21.5 us  [summed(): pl.pallas_call(body, out_shape=[jax.ShapeDtypeStruct(s, jnp.float32) for...]
  transfers between devices with their start and end apart: 32 -> 40, of which waited for: 15 -> 14; matrix products, arithmetic and copies ran while one was open for 0% -> 0% of each run, Pallas kernels for 17% -> 18%
where the time goes in v2:
time: 148 us
  waiting for transfers between devices  77.7 us (52%)
  starting transfers between devices  35.6 us (24%)
  Pallas kernels  32 us (22%)
  between operations  1.48 us (1%)
    ppermute x7, waiting for transfers between devices, ring_chunks(): fore[lane] = lax.ppermute(fore[lane], 'samp', ahead)  44.6 us
    ppermute x7, waiting for transfers between devices, wanted_rows(): came = lax.ppermute(sent[0], 'snp', across)  22.3 us
    pallas_call x7, Pallas kernels, summed(): pl.pallas_call(body, out_shape=[jax.ShapeDtypeStruct(s, jnp.float32) for...  21.5 us
    ppermute x7, starting transfers between devices, ring_chunks(): fore[lane] = lax.ppermute(fore[lane], 'samp', ahead)  11.4 us
    ppermute x7, starting transfers between devices, wanted_rows(): came = lax.ppermute(sent[0], 'snp', across)  10.7 us
    pallas_call x15, Pallas kernels, local_call(): pl.pallas_call(functools.partial(body, win_cols=win_cols), out_shape=[jax...  10.5 us
    ppermute x7, starting transfers between devices, ring_chunks(): aft[lane] = lax.ppermute(aft[lane], 'samp', back)  8 us
    ppermute x7, waiting for transfers between devices, ring_chunks(): aft[lane] = lax.ppermute(aft[lane], 'samp', back)  5.51 us
  transfers between devices with their start and end apart: 40, of which 14 were waited for; matrix products, arithmetic and copies ran while one was open for 0% of the time, Pallas kernels for 18%

profile of v2, /device:TPU:0, one launch (start us, length us, event | category | flops | bytes accessed | tf_op | source)
XLA Modules:
  0.0 148.3 jit_solution(2489253113501856533)
XLA Ops:
  3.9 2.6 %collective-permute-start.9 = (bf16[256,1024]{1,0:T(8,128)(2,1)S(1)}, bf16[256,1024]{1,0:T(8,128)(2,1)S(1)}, u32[]{:S(2)}, u32[]{:S(2)}) collective-permute-start(bf16[256,1024]{1,0:T(8,128)(2,1)S(1)} %get-tuple-element.36.refs_0_), channel_id=1, source_target_pairs={{0,8},{8,16},{16,24},{24,28},{28,20},{20,12},{12,4},{4,0},{1,9},{9... | collective-permute-start | bytes 1572872 | tf_op jit(solution)/shard_map/ppermute | solution.py:32
  6.6 2.0 %collective-permute-start = (bf16[256,1024]{1,0:T(8,128)(2,1)S(1)}, bf16[256,1024]{1,0:T(8,128)(2,1)S(1)}, u32[]{:S(2)}, u32[]{:S(2)}) collective-permute-start(bf16[256,1024]{1,0:T(8,128)(2,1)S(1)} %get-tuple-element.37.refs_1_), channel_id=1, source_target_pairs={{0,8},{8,16},{16,24},{24,28},{28,20},{20,12},{12,4},{4,0},{1,9},{9... | collective-permute-start | bytes 1572872 | tf_op jit(solution)/shard_map/ppermute | solution.py:32
  8.6 10.7 %collective-permute-done.9.refs_0_ = bf16[256,1024]{1,0:T(8,128)(2,1)S(1)} collective-permute-done((bf16[256,1024]{1,0:T(8,128)(2,1)S(1)}, bf16[256,1024]{1,0:T(8,128)(2,1)S(1)}, u32[]{:S(2)}, u32[]{:S(2)}) %collective-permute-start.9) | collective-permute-done | bytes 524320 | tf_op jit(solution)/shard_map/ppermute | solution.py:32
  19.3 2.1 %collective-permute-start.10 = (bf16[256,1024]{1,0:T(8,128)(2,1)S(1)}, bf16[256,1024]{1,0:T(8,128)(2,1)S(1)}, u32[]{:S(2)}, u32[]{:S(2)}) collective-permute-start(bf16[256,1024]{1,0:T(8,128)(2,1)S(1)} %collective-permute-done.9.refs_0_), channel_id=1, source_target_pairs={{0,8},{8,16},{16,24},{24,28},{28,20},{20,12},{12,4},{4,0},{1,9},{9... | collective-permute-start | bytes 1572872 | tf_op jit(solution)/shard_map/ppermute | solution.py:32
  24.0 6.5 %collective-permute-done.refs_0_ = bf16[256,1024]{1,0:T(8,128)(2,1)S(1)} collective-permute-done((bf16[256,1024]{1,0:T(8,128)(2,1)S(1)}, bf16[256,1024]{1,0:T(8,128)(2,1)S(1)}, u32[]{:S(2)}, u32[]{:S(2)}) %collective-permute-start) | collective-permute-done | bytes 524320 | tf_op jit(solution)/shard_map/ppermute | solution.py:32
  30.5 2.1 %collective-permute-start.1 = (bf16[256,1024]{1,0:T(8,128)(2,1)S(1)}, bf16[256,1024]{1,0:T(8,128)(2,1)S(1)}, u32[]{:S(2)}, u32[]{:S(2)}) collective-permute-start(bf16[256,1024]{1,0:T(8,128)(2,1)S(1)} %collective-permute-done.refs_0_), channel_id=1, source_target_pairs={{0,8},{8,16},{16,24},{24,28},{28,20},{20,12},{12,4},{4,0},{1,9},{9... | collective-permute-start | bytes 1572872 | tf_op jit(solution)/shard_map/ppermute | solution.py:32
  34.8 6.9 %collective-permute-done.10.refs_0_ = bf16[256,1024]{1,0:T(8,128)(2,1)S(1)} collective-permute-done((bf16[256,1024]{1,0:T(8,128)(2,1)S(1)}, bf16[256,1024]{1,0:T(8,128)(2,1)S(1)}, u32[]{:S(2)}, u32[]{:S(2)}) %collective-permute-start.10) | collective-permute-done | bytes 524320 | tf_op jit(solution)/shard_map/ppermute | solution.py:32
  41.7 2.0 %collective-permute-start.4 = (bf16[256,1024]{1,0:T(8,128)(2,1)S(1)}, bf16[256,1024]{1,0:T(8,128)(2,1)S(1)}, u32[]{:S(2)}, u32[]{:S(2)}) collective-permute-start(bf16[256,1024]{1,0:T(8,128)(2,1)S(1)} %collective-permute-done.3.refs_1_), channel_id=1, source_target_pairs={{0,4},{8,0},{16,8},{24,16},{28,24},{20,28},{12,20},{4,12},{1,5},{9... | collective-permute-start | bytes 1572872 | tf_op jit(solution)/shard_map/ppermute | solution.py:33
  44.6 8.4 %collective-permute-done.1.refs_0_ = bf16[256,1024]{1,0:T(8,128)(2,1)S(1)} collective-permute-done((bf16[256,1024]{1,0:T(8,128)(2,1)S(1)}, bf16[256,1024]{1,0:T(8,128)(2,1)S(1)}, u32[]{:S(2)}, u32[]{:S(2)}) %collective-permute-start.1) | collective-permute-done | bytes 524320 | tf_op jit(solution)/shard_map/ppermute | solution.py:32
  53.0 2.0 %collective-permute-start.15 = (bf16[256,1024]{1,0:T(8,128)(2,1)S(1)}, bf16[256,1024]{1,0:T(8,128)(2,1)S(1)}, u32[]{:S(2)}, u32[]{:S(2)}) collective-permute-start(bf16[256,1024]{1,0:T(8,128)(2,1)S(1)} %collective-permute-done.14.refs_1_), channel_id=1, source_target_pairs={{0,4},{8,0},{16,8},{24,16},{28,24},{20,28},{12,20},{4,12},{1,5},{9... | collective-permute-start | bytes 1572872 | tf_op jit(solution)/shard_map/ppermute | solution.py:33
  55.8 2.0 %collective-permute-start.35 = (bf16[1,640,256]{2,1,0:T(8,128)(2,1)S(1)}, bf16[1,640,256]{2,1,0:T(8,128)(2,1)S(1)}, u32[]{:S(2)}, u32[]{:S(2)}) collective-permute-start(bf16[1,640,256]{2,1,0:T(8,128)(2,1)S(1)} %shard_map.42), channel_id=1, source_target_pairs={{0,2},{1,3},{2,0},{3,1},{4,6},{5,7},{6,4},{7,5},{8,10},{9,11},{10,... | collective-permute-start | bytes 983048 | tf_op jit(solution)/shard_map/ppermute | solution.py:117
  57.8 6.4 %collective-permute-done.11.refs_0_ = bf16[256,1024]{1,0:T(8,128)(2,1)S(1)} collective-permute-done((bf16[256,1024]{1,0:T(8,128)(2,1)S(1)}, bf16[256,1024]{1,0:T(8,128)(2,1)S(1)}, u32[]{:S(2)}, u32[]{:S(2)}) %collective-permute-start.11) | collective-permute-done | bytes 524320 | tf_op jit(solution)/shard_map/ppermute | solution.py:32
  64.2 2.0 %collective-permute-start.5 = (bf16[256,1024]{1,0:T(8,128)(2,1)S(1)}, bf16[256,1024]{1,0:T(8,128)(2,1)S(1)}, u32[]{:S(2)}, u32[]{:S(2)}) collective-permute-start(bf16[256,1024]{1,0:T(8,128)(2,1)S(1)} %collective-permute-done.4.refs_1_), channel_id=1, source_target_pairs={{0,4},{8,0},{16,8},{24,16},{28,24},{20,28},{12,20},{4,12},{1,5},{9... | collective-permute-start | bytes 1572872 | tf_op jit(solution)/shard_map/ppermute | solution.py:33
  69.4 5.7 %collective-permute-done.2.refs_0_ = bf16[256,1024]{1,0:T(8,128)(2,1)S(1)} collective-permute-done((bf16[256,1024]{1,0:T(8,128)(2,1)S(1)}, bf16[256,1024]{1,0:T(8,128)(2,1)S(1)}, u32[]{:S(2)}, u32[]{:S(2)}) %collective-permute-start.2) | collective-permute-done | bytes 524320 | tf_op jit(solution)/shard_map/ppermute | solution.py:32
  75.8 1.9 %collective-permute-done.5.refs_1_ = bf16[256,1024]{1,0:T(8,128)(2,1)S(1)} collective-permute-done((bf16[256,1024]{1,0:T(8,128)(2,1)S(1)}, bf16[256,1024]{1,0:T(8,128)(2,1)S(1)}, u32[]{:S(2)}, u32[]{:S(2)}) %collective-permute-start.5) | collective-permute-done | bytes 524320 | tf_op jit(solution)/shard_map/ppermute | solution.py:33
  82.1 3.9 %collective-permute-done.32.refs_4_ = bf16[1,640,256]{2,1,0:T(8,128)(2,1)S(1)} collective-permute-done((bf16[1,640,256]{2,1,0:T(8,128)(2,1)S(1)}, bf16[1,640,256]{2,1,0:T(8,128)(2,1)S(1)}, u32[]{:S(2)}, u32[]{:S(2)}) %collective-permute-start.32) | collective-permute-done | bytes 327712 | tf_op jit(solution)/shard_map/ppermute | solution.py:117
  86.5 1.7 %collective-permute-start.29 = (bf16[1,640,256]{2,1,0:T(8,128)(2,1)S(1)}, bf16[1,640,256]{2,1,0:T(8,128)(2,1)S(1)}, u32[]{:S(2)}, u32[]{:S(2)}) collective-permute-start(bf16[1,640,256]{2,1,0:T(8,128)(2,1)S(1)} %shard_map.38), channel_id=1, source_target_pairs={{0,2},{1,3},{2,0},{3,1},{4,6},{5,7},{6,4},{7,5},{8,10},{9,11},{10,... | collective-permute-start | bytes 983048 | tf_op jit(solution)/shard_map/ppermute | solution.py:117
  91.1 5.1 %collective-permute-done.29.refs_4_ = bf16[1,640,256]{2,1,0:T(8,128)(2,1)S(1)} collective-permute-done((bf16[1,640,256]{2,1,0:T(8,128)(2,1)S(1)}, bf16[1,640,256]{2,1,0:T(8,128)(2,1)S(1)}, u32[]{:S(2)}, u32[]{:S(2)}) %collective-permute-start.29) | collective-permute-done | bytes 327712 | tf_op jit(solution)/shard_map/ppermute | solution.py:117
  96.2 1.7 %collective-permute-start.26 = (bf16[1,640,256]{2,1,0:T(8,128)(2,1)S(1)}, bf16[1,640,256]{2,1,0:T(8,128)(2,1)S(1)}, u32[]{:S(2)}, u32[]{:S(2)}) collective-permute-start(bf16[1,640,256]{2,1,0:T(8,128)(2,1)S(1)} %shard_map.36), channel_id=1, source_target_pairs={{0,2},{1,3},{2,0},{3,1},{4,6},{5,7},{6,4},{7,5},{8,10},{9,11},{10,... | collective-permute-start | bytes 983048 | tf_op jit(solution)/shard_map/ppermute | solution.py:117
  98.2 3.6 %collective-permute-done.16.refs_1_.refs_7_ = bf16[256,1024]{1,0:T(8,128)(2,1)S(1)} collective-permute-done((bf16[256,1024]{1,0:T(8,128)(2,1)S(1)}, bf16[256,1024]{1,0:T(8,128)(2,1)S(1)}, u32[]{:S(2)}, u32[]{:S(2)}) %collective-permute-start.16) | collective-permute-done | bytes 524320 | tf_op jit(solution)/shard_map/ppermute | solution.py:33
  104.0 2.8 %collective-permute-done.26.refs_4_ = bf16[1,640,256]{2,1,0:T(8,128)(2,1)S(1)} collective-permute-done((bf16[1,640,256]{2,1,0:T(8,128)(2,1)S(1)}, bf16[1,640,256]{2,1,0:T(8,128)(2,1)S(1)}, u32[]{:S(2)}, u32[]{:S(2)}) %collective-permute-start.26) | collective-permute-done | bytes 327712 | tf_op jit(solution)/shard_map/ppermute | solution.py:117
  108.5 5.3 %collective-permute-done.20 = bf16[1,640,256]{2,1,0:T(8,128)(2,1)S(1)} collective-permute-done((bf16[1,640,256]{2,1,0:T(8,128)(2,1)S(1)}, bf16[1,640,256]{2,1,0:T(8,128)(2,1)S(1)}, u32[]{:S(2)}, u32[]{:S(2)}) %collective-permute-start.20) | collective-permute-done | bytes 327712 | tf_op jit(solution)/shard_map/ppermute | solution.py:115
  113.8 1.8 %collective-permute-start.21 = (bf16[1,640,256]{2,1,0:T(8,128)(2,1)S(1)}, bf16[1,640,256]{2,1,0:T(8,128)(2,1)S(1)}, u32[]{:S(2)}, u32[]{:S(2)}) collective-permute-start(bf16[1,640,256]{2,1,0:T(8,128)(2,1)S(1)} %collective-permute-done.20), channel_id=1, source_target_pairs={{0,8},{2,10},{8,16},{10,18},{16,24},{18,26},{24,28},{26,30},{28,20... | collective-permute-start | bytes 983048 | tf_op jit(solution)/shard_map/ppermute | solution.py:116
  115.6 5.2 %collective-permute-done.23.refs_4_ = bf16[1,640,256]{2,1,0:T(8,128)(2,1)S(1)} collective-permute-done((bf16[1,640,256]{2,1,0:T(8,128)(2,1)S(1)}, bf16[1,640,256]{2,1,0:T(8,128)(2,1)S(1)}, u32[]{:S(2)}, u32[]{:S(2)}) %collective-permute-start.23) | collective-permute-done | bytes 327712 | tf_op jit(solution)/shard_map/ppermute | solution.py:117
  120.8 5.3 %collective-permute-done.7.refs_4_ = bf16[1,640,256]{2,1,0:T(8,128)(2,1)S(1)} collective-permute-done((bf16[1,640,256]{2,1,0:T(8,128)(2,1)S(1)}, bf16[1,640,256]{2,1,0:T(8,128)(2,1)S(1)}, u32[]{:S(2)}, u32[]{:S(2)}) %collective-permute-start.7) | collective-permute-done | bytes 327712 | tf_op jit(solution)/shard_map/ppermute | solution.py:117
  126.6 2.6 %shard_map.45 = (f32[640,1024]{1,0:T(8,128)S(1)}, f32[16,1024]{1,0:T(8,128)S(1)}, f32[2,640,128]{2,1,0:T(8,128)S(1)}) custom-call(s32[8]{0:T(128)S(1)} %stack.75.where, bf16[256,1024]{1,0:T(8,128)(2,1)S(1)} %get-tuple-element.36.refs_0_, bf16[256,1024]{1,0:T(8,128)(2,1)S(1)} %get-tuple-element.37.refs_1_, ...), custom_call_target="tpu_custom_call" | custom-call | tf_op jit(solution)/shard_map/pallas_call | solution.py:277
  129.2 2.8 %shard_map.46 = (f32[640,1024]{1,0:T(8,128)S(1)}, f32[16,1024]{1,0:T(8,128)S(1)}, f32[2,640,128]{2,1,0:T(8,128)S(1)}) custom-call(s32[8]{0:T(128)S(1)} %stack.75.where, bf16[256,1024]{1,0:T(8,128)(2,1)S(1)} %collective-permute-done.9.refs_0_, ...), custom_call_target="tpu_custom_call", output_to_operand_aliasing={{0}: (7, {}), {1}: (8, {}), {2}: (9, {})} | custom-call | tf_op jit(solution)/shard_map/pallas_call | solution.py:277
  132.0 2.8 %shard_map.47 = (f32[640,1024]{1,0:T(8,128)S(1)}, f32[16,1024]{1,0:T(8,128)S(1)}, f32[2,640,128]{2,1,0:T(8,128)S(1)}) custom-call(s32[8]{0:T(128)S(1)} %stack.75.where, bf16[256,1024]{1,0:T(8,128)(2,1)S(1)} %collective-permute-done.refs_0_, ...), custom_call_target="tpu_custom_call", output_to_operand_aliasing={{0}: (7, {}), {1}: (8, {}), {2}: (9, {})} | custom-call | tf_op jit(solution)/shard_map/pallas_call | solution.py:277
  134.8 2.8 %shard_map.48 = (f32[640,1024]{1,0:T(8,128)S(1)}, f32[16,1024]{1,0:T(8,128)S(1)}, f32[2,640,128]{2,1,0:T(8,128)S(1)}) custom-call(s32[8]{0:T(128)S(1)} %stack.75.where, bf16[256,1024]{1,0:T(8,128)(2,1)S(1)} %collective-permute-done.10.refs_0_, ...), custom_call_target="tpu_custom_call", output_to_operand_aliasing={{0}: (7, {}), {1}: (8, {}), {2}: (9, {})} | custom-call | tf_op jit(solution)/shard_map/pallas_call | solution.py:277
  137.6 3.0 %shard_map.49 = (f32[640,1024]{1,0:T(8,128)S(1)}, f32[16,1024]{1,0:T(8,128)S(1)}, f32[2,640,128]{2,1,0:T(8,128)S(1)}) custom-call(s32[8]{0:T(128)S(1)} %stack.75.where, bf16[256,1024]{1,0:T(8,128)(2,1)S(1)} %collective-permute-done.1.refs_0_, ...), custom_call_target="tpu_custom_call", output_to_operand_aliasing={{0}: (7, {}), {1}: (8, {}), {2}: (9, {})} | custom-call | tf_op jit(solution)/shard_map/pallas_call | solution.py:277
  140.6 2.8 %shard_map.50 = (f32[640,1024]{1,0:T(8,128)S(1)}, f32[16,1024]{1,0:T(8,128)S(1)}, f32[2,640,128]{2,1,0:T(8,128)S(1)}) custom-call(s32[8]{0:T(128)S(1)} %stack.75.where, bf16[256,1024]{1,0:T(8,128)(2,1)S(1)} %collective-permute-done.11.refs_0_, ...), custom_call_target="tpu_custom_call", output_to_operand_aliasing={{0}: (7, {}), {1}: (8, {}), {2}: (9, {})} | custom-call | tf_op jit(solution)/shard_map/pallas_call | solution.py:277
  143.4 4.8 %shard_map.51 = (f32[512,1024]{1,0:T(8,128)}, f32[128,1024]{1,0:T(8,128)}) custom-call(s32[8]{0:T(128)S(1)} %stack.75.where, bf16[256,1024]{1,0:T(8,128)(2,1)S(1)} %collective-permute-done.2.refs_0_, bf16[256,1024]{1,0:T(8,128)(2,1)S(1)} %collective-permute-done.5.refs_1_, bf16[2,640,256]{2,1,0:T(8,128)(2,1)S(1)} %shard_map.30.refs_0_.refs_2_, ...), custom_call_target="tpu_custom_call" | custom-call | tf_op jit(solution)/shard_map/pallas_call | solution.py:277
  (73 shorter events, 25.4 us)
Async XLA Ops:
  3.4 18.0 %collective-permute-start.37 = (bf16[2,640,256]{2,1,0:T(8,128)(2,1)S(1)}, bf16[2,640,256]{2,1,0:T(8,128)(2,1)S(1)}, u32[]{:S(2)}, u32[]{:S(2)}) collective-permute-start(bf16[2,640,256]{2,1,0:T(8,128)(2,1)S(1)} %shard_map.43.refs_0_.refs_2_), channel_id=1, source_target_pairs={{0,1},{1,0},{2,3},{3,2},{4,5},{5,4},{6,7},{7,6},{8,9},{9,8},{10,11... | collective-permute-start | bytes 1966088 | tf_op jit(solution)/shard_map/ppermute | solution.py:106
  3.9 15.3 %collective-permute-start.9 = (bf16[256,1024]{1,0:T(8,128)(2,1)S(1)}, bf16[256,1024]{1,0:T(8,128)(2,1)S(1)}, u32[]{:S(2)}, u32[]{:S(2)}) collective-permute-start(bf16[256,1024]{1,0:T(8,128)(2,1)S(1)} %get-tuple-element.36.refs_0_), channel_id=1, source_target_pairs={{0,8},{8,16},{16,24},{24,28},{28,20},{20,12},{12,4},{4,0},{1,9},{9... | collective-permute-start | bytes 1572872 | tf_op jit(solution)/shard_map/ppermute | solution.py:32
  6.6 17.0 %collective-permute-start.13 = (bf16[256,1024]{1,0:T(8,128)(2,1)S(1)}, bf16[256,1024]{1,0:T(8,128)(2,1)S(1)}, u32[]{:S(2)}, u32[]{:S(2)}) collective-permute-start(bf16[256,1024]{1,0:T(8,128)(2,1)S(1)} %get-tuple-element.37.refs_1_), channel_id=1, source_target_pairs={{0,4},{8,0},{16,8},{24,16},{28,24},{20,28},{12,20},{4,12},{1,5},{9... | collective-permute-start | bytes 1572872 | tf_op jit(solution)/shard_map/ppermute | solution.py:33
  6.6 23.9 %collective-permute-start = (bf16[256,1024]{1,0:T(8,128)(2,1)S(1)}, bf16[256,1024]{1,0:T(8,128)(2,1)S(1)}, u32[]{:S(2)}, u32[]{:S(2)}) collective-permute-start(bf16[256,1024]{1,0:T(8,128)(2,1)S(1)} %get-tuple-element.37.refs_1_), channel_id=1, source_target_pairs={{0,8},{8,16},{16,24},{24,28},{28,20},{20,12},{12,4},{4,0},{1,9},{9... | collective-permute-start | bytes 1572872 | tf_op jit(solution)/shard_map/ppermute | solution.py:32
  8.6 24.8 %collective-permute-start.3 = (bf16[256,1024]{1,0:T(8,128)(2,1)S(1)}, bf16[256,1024]{1,0:T(8,128)(2,1)S(1)}, u32[]{:S(2)}, u32[]{:S(2)}) collective-permute-start(bf16[256,1024]{1,0:T(8,128)(2,1)S(1)} %get-tuple-element.36.refs_0_), channel_id=1, source_target_pairs={{0,4},{8,0},{16,8},{24,16},{28,24},{20,28},{12,20},{4,12},{1,5},{9... | collective-permute-start | bytes 1572872 | tf_op jit(solution)/shard_map/ppermute | solution.py:33
  19.3 22.5 %collective-permute-start.10 = (bf16[256,1024]{1,0:T(8,128)(2,1)S(1)}, bf16[256,1024]{1,0:T(8,128)(2,1)S(1)}, u32[]{:S(2)}, u32[]{:S(2)}) collective-permute-start(bf16[256,1024]{1,0:T(8,128)(2,1)S(1)} %collective-permute-done.9.refs_0_), channel_id=1, source_target_pairs={{0,8},{8,16},{16,24},{24,28},{28,20},{20,12},{12,4},{4,0},{1,9},{9... | collective-permute-start | bytes 1572872 | tf_op jit(solution)/shard_map/ppermute | solution.py:32
  23.6 20.2 %collective-permute-start.14 = (bf16[256,1024]{1,0:T(8,128)(2,1)S(1)}, bf16[256,1024]{1,0:T(8,128)(2,1)S(1)}, u32[]{:S(2)}, u32[]{:S(2)}) collective-permute-start(bf16[256,1024]{1,0:T(8,128)(2,1)S(1)} %collective-permute-done.13.refs_1_), channel_id=1, source_target_pairs={{0,4},{8,0},{16,8},{24,16},{28,24},{20,28},{12,20},{4,12},{1,5},{9... | collective-permute-start | bytes 1572872 | tf_op jit(solution)/shard_map/ppermute | solution.py:33
  30.5 22.5 %collective-permute-start.1 = (bf16[256,1024]{1,0:T(8,128)(2,1)S(1)}, bf16[256,1024]{1,0:T(8,128)(2,1)S(1)}, u32[]{:S(2)}, u32[]{:S(2)}) collective-permute-start(bf16[256,1024]{1,0:T(8,128)(2,1)S(1)} %collective-permute-done.refs_0_), channel_id=1, source_target_pairs={{0,8},{8,16},{16,24},{24,28},{28,20},{20,12},{12,4},{4,0},{1,9},{9... | collective-permute-start | bytes 1572872 | tf_op jit(solution)/shard_map/ppermute | solution.py:32
  33.4 21.6 %collective-permute-start.34 = (bf16[2,640,256]{2,1,0:T(8,128)(2,1)S(1)}, bf16[2,640,256]{2,1,0:T(8,128)(2,1)S(1)}, u32[]{:S(2)}, u32[]{:S(2)}) collective-permute-start(bf16[2,640,256]{2,1,0:T(8,128)(2,1)S(1)} %shard_map.41.refs_0_.refs_2_), channel_id=1, source_target_pairs={{0,1},{1,0},{2,3},{3,2},{4,5},{5,4},{6,7},{7,6},{8,9},{9,8},{10,11... | collective-permute-start | bytes 1966088 | tf_op jit(solution)/shard_map/ppermute | solution.py:106
  34.2 21.5 %collective-permute-start.31 = (bf16[2,640,256]{2,1,0:T(8,128)(2,1)S(1)}, bf16[2,640,256]{2,1,0:T(8,128)(2,1)S(1)}, u32[]{:S(2)}, u32[]{:S(2)}) collective-permute-start(bf16[2,640,256]{2,1,0:T(8,128)(2,1)S(1)} %shard_map.39.refs_0_.refs_2_), channel_id=1, source_target_pairs={{0,1},{1,0},{2,3},{3,2},{4,5},{5,4},{6,7},{7,6},{8,9},{9,8},{10,11... | collective-permute-start | bytes 1966088 | tf_op jit(solution)/shard_map/ppermute | solution.py:106
  41.7 14.0 %collective-permute-start.4 = (bf16[256,1024]{1,0:T(8,128)(2,1)S(1)}, bf16[256,1024]{1,0:T(8,128)(2,1)S(1)}, u32[]{:S(2)}, u32[]{:S(2)}) collective-permute-start(bf16[256,1024]{1,0:T(8,128)(2,1)S(1)} %collective-permute-done.3.refs_1_), channel_id=1, source_target_pairs={{0,4},{8,0},{16,8},{24,16},{28,24},{20,28},{12,20},{4,12},{1,5},{9... | collective-permute-start | bytes 1572872 | tf_op jit(solution)/shard_map/ppermute | solution.py:33
  43.7 20.4 %collective-permute-start.11 = (bf16[256,1024]{1,0:T(8,128)(2,1)S(1)}, bf16[256,1024]{1,0:T(8,128)(2,1)S(1)}, u32[]{:S(2)}, u32[]{:S(2)}) collective-permute-start(bf16[256,1024]{1,0:T(8,128)(2,1)S(1)} %collective-permute-done.10.refs_0_), channel_id=1, source_target_pairs={{0,8},{8,16},{16,24},{24,28},{28,20},{20,12},{12,4},{4,0},{1,9},{9... | collective-permute-start | bytes 1572872 | tf_op jit(solution)/shard_map/ppermute | solution.py:32
  53.0 14.0 %collective-permute-start.15 = (bf16[256,1024]{1,0:T(8,128)(2,1)S(1)}, bf16[256,1024]{1,0:T(8,128)(2,1)S(1)}, u32[]{:S(2)}, u32[]{:S(2)}) collective-permute-start(bf16[256,1024]{1,0:T(8,128)(2,1)S(1)} %collective-permute-done.14.refs_1_), channel_id=1, source_target_pairs={{0,4},{8,0},{16,8},{24,16},{28,24},{20,28},{12,20},{4,12},{1,5},{9... | collective-permute-start | bytes 1572872 | tf_op jit(solution)/shard_map/ppermute | solution.py:33
  55.0 20.2 %collective-permute-start.2 = (bf16[256,1024]{1,0:T(8,128)(2,1)S(1)}, bf16[256,1024]{1,0:T(8,128)(2,1)S(1)}, u32[]{:S(2)}, u32[]{:S(2)}) collective-permute-start(bf16[256,1024]{1,0:T(8,128)(2,1)S(1)} %collective-permute-done.1.refs_0_), channel_id=1, source_target_pairs={{0,8},{8,16},{16,24},{24,28},{28,20},{20,12},{12,4},{4,0},{1,9},{9... | collective-permute-start | bytes 1572872 | tf_op jit(solution)/shard_map/ppermute | solution.py:32
  55.7 13.1 %collective-permute-start.39 = (bf16[1,640,256]{2,1,0:T(8,128)(2,1)S(1)}, bf16[1,640,256]{2,1,0:T(8,128)(2,1)S(1)}, u32[]{:S(2)}, u32[]{:S(2)}) collective-permute-start(bf16[1,640,256]{2,1,0:T(8,128)(2,1)S(1)} %collective-permute-done.38.refs_4_), channel_id=1, source_target_pairs={{0,1},{1,0},{2,3},{3,2},{4,5},{5,4},{6,7},{7,6},{8,9},{9,8},{10,11... | collective-permute-start | bytes 983048 | tf_op jit(solution)/shard_map/ppermute | solution.py:118
  55.8 13.6 %collective-permute-start.35 = (bf16[1,640,256]{2,1,0:T(8,128)(2,1)S(1)}, bf16[1,640,256]{2,1,0:T(8,128)(2,1)S(1)}, u32[]{:S(2)}, u32[]{:S(2)}) collective-permute-start(bf16[1,640,256]{2,1,0:T(8,128)(2,1)S(1)} %shard_map.42), channel_id=1, source_target_pairs={{0,2},{1,3},{2,0},{3,1},{4,6},{5,7},{6,4},{7,5},{8,10},{9,11},{10,... | collective-permute-start | bytes 983048 | tf_op jit(solution)/shard_map/ppermute | solution.py:117
  64.2 13.4 %collective-permute-start.5 = (bf16[256,1024]{1,0:T(8,128)(2,1)S(1)}, bf16[256,1024]{1,0:T(8,128)(2,1)S(1)}, u32[]{:S(2)}, u32[]{:S(2)}) collective-permute-start(bf16[256,1024]{1,0:T(8,128)(2,1)S(1)} %collective-permute-done.4.refs_1_), channel_id=1, source_target_pairs={{0,4},{8,0},{16,8},{24,16},{28,24},{20,28},{12,20},{4,12},{1,5},{9... | collective-permute-start | bytes 1572872 | tf_op jit(solution)/shard_map/ppermute | solution.py:33
  68.8 17.2 %collective-permute-start.25 = (bf16[2,640,256]{2,1,0:T(8,128)(2,1)S(1)}, bf16[2,640,256]{2,1,0:T(8,128)(2,1)S(1)}, u32[]{:S(2)}, u32[]{:S(2)}) collective-permute-start(bf16[2,640,256]{2,1,0:T(8,128)(2,1)S(1)} %shard_map.35.refs_0_.refs_2_), channel_id=1, source_target_pairs={{0,1},{1,0},{2,3},{3,2},{4,5},{5,4},{6,7},{7,6},{8,9},{9,8},{10,11... | collective-permute-start | bytes 1966088 | tf_op jit(solution)/shard_map/ppermute | solution.py:106
  69.4 17.2 %collective-permute-start.18 = (bf16[2,640,256]{2,1,0:T(8,128)(2,1)S(1)}, bf16[2,640,256]{2,1,0:T(8,128)(2,1)S(1)}, u32[]{:S(2)}, u32[]{:S(2)}) collective-permute-start(bf16[2,640,256]{2,1,0:T(8,128)(2,1)S(1)} %get-tuple-element.32.refs_0_.refs_2_), channel_id=1, source_target_pairs={{0,1},{1,0},{2,3},{3,2},{4,5},{5,4},{6,7},{7,6},{8,9},{9,8},{10,11... | collective-permute-start | bytes 1966088 | tf_op jit(solution)/shard_map/ppermute | solution.py:106
  75.2 13.1 %collective-permute-start.19 = (bf16[2,640,256]{2,1,0:T(8,128)(2,1)S(1)}, bf16[2,640,256]{2,1,0:T(8,128)(2,1)S(1)}, u32[]{:S(2)}, u32[]{:S(2)}) collective-permute-start(bf16[2,640,256]{2,1,0:T(8,128)(2,1)S(1)} %get-tuple-element.33.refs_2_), channel_id=1, source_target_pairs={{0,1},{1,0},{2,3},{3,2},{4,5},{5,4},{6,7},{7,6},{8,9},{9,8},{10,11... | collective-permute-start | bytes 1966088 | tf_op jit(solution)/shard_map/ppermute | solution.py:111
  79.1 18.8 %collective-permute-start.12 = (bf16[256,1024]{1,0:T(8,128)(2,1)S(1)}, bf16[256,1024]{1,0:T(8,128)(2,1)S(1)}, u32[]{:S(2)}, u32[]{:S(2)}) collective-permute-start(bf16[256,1024]{1,0:T(8,128)(2,1)S(1)} %collective-permute-done.11.refs_0_), channel_id=1, source_target_pairs={{0,8},{8,16},{16,24},{24,28},{28,20},{20,12},{12,4},{4,0},{1,9},{9... | collective-permute-start | bytes 1572872 | tf_op jit(solution)/shard_map/ppermute | solution.py:32
  86.0 16.7 %collective-permute-start.6 = (bf16[2,640,256]{2,1,0:T(8,128)(2,1)S(1)}, bf16[2,640,256]{2,1,0:T(8,128)(2,1)S(1)}, u32[]{:S(2)}, u32[]{:S(2)}) collective-permute-start(bf16[2,640,256]{2,1,0:T(8,128)(2,1)S(1)} %shard_map.30.refs_0_.refs_2_), channel_id=1, source_target_pairs={{0,1},{1,0},{2,3},{3,2},{4,5},{5,4},{6,7},{7,6},{8,9},{9,8},{10,11... | collective-permute-start | bytes 1966088 | tf_op jit(solution)/shard_map/ppermute | solution.py:106
  88.3 13.6 %collective-permute-start.16 = (bf16[256,1024]{1,0:T(8,128)(2,1)S(1)}, bf16[256,1024]{1,0:T(8,128)(2,1)S(1)}, u32[]{:S(2)}, u32[]{:S(2)}) collective-permute-start(bf16[256,1024]{1,0:T(8,128)(2,1)S(1)} %collective-permute-done.15.refs_1_), channel_id=1, source_target_pairs={{0,4},{8,0},{16,8},{24,16},{28,24},{20,28},{12,20},{4,12},{1,5},{9... | collective-permute-start | bytes 1572872 | tf_op jit(solution)/shard_map/ppermute | solution.py:33
  98.0 15.9 %collective-permute-start.20 = (bf16[1,640,256]{2,1,0:T(8,128)(2,1)S(1)}, bf16[1,640,256]{2,1,0:T(8,128)(2,1)S(1)}, u32[]{:S(2)}, u32[]{:S(2)}) collective-permute-start(bf16[1,640,256]{2,1,0:T(8,128)(2,1)S(1)} %get-tuple-element.34), channel_id=1, source_target_pairs={{0,2},{1,3},{2,0},{3,1},{4,6},{5,7},{6,4},{7,5},{8,10},{9,11},{10,... | collective-permute-start | bytes 983048 | tf_op jit(solution)/shard_map/ppermute | solution.py:115
  101.9 13.7 %collective-permute-start.30 = (bf16[1,640,256]{2,1,0:T(8,128)(2,1)S(1)}, bf16[1,640,256]{2,1,0:T(8,128)(2,1)S(1)}, u32[]{:S(2)}, u32[]{:S(2)}) collective-permute-start(bf16[1,640,256]{2,1,0:T(8,128)(2,1)S(1)} %collective-permute-done.29.refs_4_), channel_id=1, source_target_pairs={{0,1},{1,0},{2,3},{3,2},{4,5},{5,4},{6,7},{7,6},{8,9},{9,8},{10,11... | collective-permute-start | bytes 983048 | tf_op jit(solution)/shard_map/ppermute | solution.py:118
  102.7 18.2 %collective-permute-start.23 = (bf16[1,640,256]{2,1,0:T(8,128)(2,1)S(1)}, bf16[1,640,256]{2,1,0:T(8,128)(2,1)S(1)}, u32[]{:S(2)}, u32[]{:S(2)}) collective-permute-start(bf16[1,640,256]{2,1,0:T(8,128)(2,1)S(1)} %get-tuple-element.35), channel_id=1, source_target_pairs={{0,2},{1,3},{2,0},{3,1},{4,6},{5,7},{6,4},{7,5},{8,10},{9,11},{10,... | collective-permute-start | bytes 983048 | tf_op jit(solution)/shard_map/ppermute | solution.py:117
  103.7 39.7 %collective-permute-start.17 = (bf16[2,640,256]{2,1,0:T(8,128)(2,1)S(1)}, bf16[2,640,256]{2,1,0:T(8,128)(2,1)S(1)}, u32[]{:S(2)}, u32[]{:S(2)}) collective-permute-start(bf16[2,640,256]{2,1,0:T(8,128)(2,1)S(1)} %shard_map.32.refs_8_), channel_id=1, source_target_pairs={{0,1},{1,0},{2,3},{3,2},{4,5},{5,4},{6,7},{7,6},{8,9},{9,8},{10,11... | collective-permute-start | bytes 1966088 | tf_op jit(solution)/shard_map/ppermute | solution.py:106
  106.8 19.3 %collective-permute-start.7 = (bf16[1,640,256]{2,1,0:T(8,128)(2,1)S(1)}, bf16[1,640,256]{2,1,0:T(8,128)(2,1)S(1)}, u32[]{:S(2)}, u32[]{:S(2)}) collective-permute-start(bf16[1,640,256]{2,1,0:T(8,128)(2,1)S(1)} %shard_map.31), channel_id=1, source_target_pairs={{0,2},{1,3},{2,0},{3,1},{4,6},{5,7},{6,4},{7,5},{8,10},{9,11},{10,... | collective-permute-start | bytes 983048 | tf_op jit(solution)/shard_map/ppermute | solution.py:117
  115.6 22.0 %collective-permute-start.27 = (bf16[1,640,256]{2,1,0:T(8,128)(2,1)S(1)}, bf16[1,640,256]{2,1,0:T(8,128)(2,1)S(1)}, u32[]{:S(2)}, u32[]{:S(2)}) collective-permute-start(bf16[1,640,256]{2,1,0:T(8,128)(2,1)S(1)} %collective-permute-done.26.refs_4_), channel_id=1, source_target_pairs={{0,1},{1,0},{2,3},{3,2},{4,5},{5,4},{6,7},{7,6},{8,9},{9,8},{10,11... | collective-permute-start | bytes 983048 | tf_op jit(solution)/shard_map/ppermute | solution.py:118
  120.8 19.8 %collective-permute-start.24 = (bf16[1,640,256]{2,1,0:T(8,128)(2,1)S(1)}, bf16[1,640,256]{2,1,0:T(8,128)(2,1)S(1)}, u32[]{:S(2)}, u32[]{:S(2)}) collective-permute-start(bf16[1,640,256]{2,1,0:T(8,128)(2,1)S(1)} %collective-permute-done.23.refs_4_), channel_id=1, source_target_pairs={{0,1},{1,0},{2,3},{3,2},{4,5},{5,4},{6,7},{7,6},{8,9},{9,8},{10,11... | collective-permute-start | bytes 983048 | tf_op jit(solution)/shard_map/ppermute | solution.py:118
  126.1 17.3 %collective-permute-start.8 = (bf16[1,640,256]{2,1,0:T(8,128)(2,1)S(1)}, bf16[1,640,256]{2,1,0:T(8,128)(2,1)S(1)}, u32[]{:S(2)}, u32[]{:S(2)}) collective-permute-start(bf16[1,640,256]{2,1,0:T(8,128)(2,1)S(1)} %collective-permute-done.7.refs_4_), channel_id=1, source_target_pairs={{0,1},{1,0},{2,3},{3,2},{4,5},{5,4},{6,7},{7,6},{8,9},{9,8},{10,11... | collective-permute-start | bytes 983048 | tf_op jit(solution)/shard_map/ppermute | solution.py:118
  126.1 17.3 %collective-permute-start.22 = (bf16[1,640,256]{2,1,0:T(8,128)(2,1)S(1)}, bf16[1,640,256]{2,1,0:T(8,128)(2,1)S(1)}, u32[]{:S(2)}, u32[]{:S(2)}) collective-permute-start(bf16[1,640,256]{2,1,0:T(8,128)(2,1)S(1)} %collective-permute-done.21.refs_10_), channel_id=1, source_target_pairs={{0,1},{1,0},{2,3},{3,2},{4,5},{5,4},{6,7},{7,6},{8,9},{9,8},{10,11... | collective-permute-start | bytes 983048 | tf_op jit(solution)/shard_map/ppermute | solution.py:118
  (8 other events, 83.0 us)
